TPU v7x, 32 devices: a whole 2x2x4 slice. The times are simulated.
32 devices in a mesh: rep: 4 (over x, core), shard: 8 (over z, y).
Axes of the slice: x: 2, y: 2, z: 4, core: 2. Of those that a mesh axis runs over, the one named last changes fastest.
Arguments:
- inputs: bfloat16 [32, 1024, 1024], P(('rep', 'shard')), may hold values from -6 to 6
- cotangent: bfloat16 [32, 1024, 1024], P(('rep', 'shard')), may hold values from -6 to 6
- lengths: int32 [32], P(('rep', 'shard')), may hold values from 256 to 1024, as said below
- adapter_ids: int32 [32], P(('rep', 'shard')), may hold values from 0 to 7
- gain_one: float32 [1024], replicated, may hold values from 0.25 to 1.75
- gain_two: float32 [1024], replicated, may hold values from 0.25 to 1.75
- qkv_weight: bfloat16 [1024, 3072], P('shard'), may hold values from -0.1875 to 0.1875
- out_weight: bfloat16 [1024, 1024], P('shard'), may hold values from -0.75 to 0.75
- up_weight: bfloat16 [1024, 4096], P('shard'), may hold values from -0.1875 to 0.1875
- down_weight: bfloat16 [4096, 1024], P('shard'), may hold values from -0.09375 to 0.09375
- adapter_down: bfloat16 [1024, 512], P('shard'), may hold values from -0.1875 to 0.1875
- adapter_up: bfloat16 [1024, 512], P('shard'), may hold values from -1.5 to 1.5
Outputs:
- layer_output: bfloat16 [32, 1024, 1024], P(('rep', 'shard'))
- input_grad: bfloat16 [32, 1024, 1024], P(('rep', 'shard'))
- adapter_down_grad: float32 [1024, 512], P('shard')
- adapter_up_grad: float32 [1024, 512], P('shard')
Inputs may be any that keep to these rules, and one draw needn't show every extreme that they name: `lengths`: every draw has a slot of length 1024.
All inputs are finite; a program needn't handle non-finite values.
Results may differ from a plain program's by a relative error of at most 0.015.
The roundings to bfloat16 on the way count: a program that leaves them out, or rounds other values in their place, can miss the bound.
Values may be sent and summed in bfloat16 or wider, within the bound.
A program may use at most 256 MiB of HBM per device.

v0:
```python
import jax
import jax.numpy as jnp
from jax import lax
from jax.sharding import PartitionSpec as P

HEADS = 16
RANK = 16
ADAPTERS = 8


EPS = 1e-05
HIGH = lax.Precision.HIGHEST


def layer_norm(vector, gain):
    center = vector - jnp.mean(vector, axis=-1, keepdims=True)
    spread = jnp.mean(center * center, axis=-1, keepdims=True)
    return center * lax.rsqrt(spread + EPS) * gain


def norm_back(vector, gain, grad_normed):

    def apply_norm(values_in):
        return layer_norm(values_in, gain)

    pull = jax.vjp(apply_norm, vector)[1]
    return pull(grad_normed)[0]


def gelu_tanh(values_in):
    return jax.nn.gelu(values_in, approximate=True)


def gelu_back(pre, grad_active):
    pull = jax.vjp(gelu_tanh, pre)[1]
    return pull(grad_active)[0]


def dense(left, right):
    return jnp.dot(left, right, preferred_element_type=jnp.float32)


def dense_trans(left, right):
    return lax.dot_general(
        left, right, (((1,), (1,)), ((), ())), preferred_element_type=jnp.float32
    )


def dense_left(left, right):
    return lax.dot_general(
        left, right, (((0,), (0,)), ((), ())), preferred_element_type=jnp.float32
    )


def split_heads(projected):
    seq = projected.shape[0]
    width = projected.shape[1] // 3
    head_size = width // HEADS
    queries = projected[:, :width].reshape(seq, HEADS, head_size)
    keys_all = projected[:, width : 2 * width].reshape(seq, HEADS, head_size)
    values_all = projected[:, 2 * width :].reshape(seq, HEADS, head_size)
    return (queries, keys_all, values_all, head_size ** (-0.5))


def block_scores(queries, keys_all, start, block, scale):
    stop = start + block
    scores = (
        jnp.einsum(
            "qhd,khd->hqk", queries[start:stop], keys_all[:stop], preferred_element_type=jnp.float32
        )
        * scale
    )
    rows = start + lax.iota(jnp.int32, block)
    causal = rows[:, None] >= lax.iota(jnp.int32, stop)[None, :]
    return (scores, causal[None])


def attention_forward(projected):
    queries, keys_all, values_all, scale = split_heads(projected)
    seq = projected.shape[0]
    block = min(512, seq)
    pieces = []
    totals = []
    for start in range(0, seq, block):
        scores, causal = block_scores(queries, keys_all, start, block, scale)
        scores = jnp.where(causal, scores, -1e30)
        peak = jnp.max(scores, axis=-1, keepdims=True)
        expo = jnp.exp(scores - peak)
        total = jnp.sum(expo, axis=-1, keepdims=True)
        probs_low = (expo / total).astype(jnp.bfloat16)
        pieces.append(
            jnp.einsum(
                "hqk,khd->qhd",
                probs_low,
                values_all[: start + block],
                preferred_element_type=jnp.float32,
            )
        )
        totals.append(peak + jnp.log(total))
    context = jnp.concatenate(pieces, axis=0).reshape(seq, -1)
    return (context, jnp.concatenate(totals, axis=1))


def attention_backward(projected, log_total, grad_context):
    queries, keys_all, values_all, scale = split_heads(projected)
    seq = projected.shape[0]
    block = min(512, seq)
    grad_ctx = grad_context.reshape(queries.shape)
    grad_keys = jnp.zeros(queries.shape, jnp.float32)
    grad_values = jnp.zeros(queries.shape, jnp.float32)
    grad_queries = []
    for start in range(0, seq, block):
        stop = start + block
        scores, causal = block_scores(queries, keys_all, start, block, scale)
        probs = jnp.where(causal, jnp.exp(scores - log_total[:, start:stop]), 0.0)
        probs_low = probs.astype(jnp.bfloat16)
        ctx_block = grad_ctx[start:stop]
        grad_values = grad_values.at[:stop].add(
            jnp.einsum("hqk,qhd->khd", probs_low, ctx_block, preferred_element_type=jnp.float32)
        )
        grad_probs = jnp.einsum(
            "qhd,khd->hqk", ctx_block, values_all[:stop], preferred_element_type=jnp.float32
        )
        grad_scores = (
            probs * (grad_probs - jnp.sum(probs * grad_probs, axis=-1, keepdims=True))
        ).astype(jnp.bfloat16)
        grad_queries.append(
            jnp.einsum(
                "hqk,khd->qhd", grad_scores, keys_all[:stop], preferred_element_type=jnp.float32
            )
            * scale
        )
        grad_keys = grad_keys.at[:stop].add(
            jnp.einsum(
                "hqk,qhd->khd", grad_scores, queries[start:stop], preferred_element_type=jnp.float32
            )
            * scale
        )
    grad_q = jnp.concatenate(grad_queries, axis=0).reshape(seq, -1)
    return jnp.concatenate(
        [grad_q, grad_keys.reshape(seq, -1), grad_values.reshape(seq, -1)], axis=1
    )


def adapter_columns(weights, adapter):
    first = adapter * (4 * RANK)
    local_down = lax.dynamic_slice_in_dim(weights[4], first, 4 * RANK, 1)
    local_up = lax.dynamic_slice_in_dim(weights[5], first, 4 * RANK, 1)
    return (local_down, local_up)


def forward_slot(tokens, length, adapter, weights, gain_one, gain_two):
    qkv_weight, out_weight, up_weight, down_weight = (
        weights[0],
        weights[1],
        weights[2],
        weights[3],
    )
    local_down, local_up = adapter_columns(weights, adapter)
    seq = tokens.shape[0]
    token_vals = tokens.astype(jnp.float32)
    normed = layer_norm(token_vals, gain_one).astype(jnp.bfloat16)
    inner = dense(normed, local_down[:, : 3 * RANK]).astype(jnp.bfloat16)
    extra = jnp.concatenate(
        [
            dense_trans(inner[:, j * RANK : (j + 1) * RANK], local_up[:, j * RANK : (j + 1) * RANK])
            for j in range(3)
        ],
        axis=1,
    )
    projected = (dense(normed, qkv_weight) + extra).astype(jnp.bfloat16)
    context, log_total = attention_forward(projected)
    context_low = context.astype(jnp.bfloat16)
    inner_out = dense(context_low, local_down[:, 3 * RANK :]).astype(jnp.bfloat16)
    hidden = token_vals + (
        dense(context_low, out_weight) + dense_trans(inner_out, local_up[:, 3 * RANK :])
    )
    normed_two = layer_norm(hidden, gain_two).astype(jnp.bfloat16)
    pre = dense(normed_two, up_weight)
    active = gelu_tanh(pre).astype(jnp.bfloat16)
    mlp = dense(active, down_weight)
    valid = (lax.iota(jnp.int32, seq) < length).astype(jnp.float32)[:, None]
    output = ((hidden + mlp) * valid).astype(jnp.bfloat16)
    return (output, (normed, inner, projected, log_total, context_low, inner_out, hidden, pre))


def backward_slot(tokens, slot_cot, length, adapter, saved, weights, gain_one, gain_two):
    qkv_weight, out_weight, up_weight, down_weight = (
        weights[0],
        weights[1],
        weights[2],
        weights[3],
    )
    local_down, local_up = adapter_columns(weights, adapter)
    normed, inner, projected, log_total, context_low, inner_out, hidden, pre = saved
    seq = tokens.shape[0]
    width = projected.shape[1] // 3
    valid = (lax.iota(jnp.int32, seq) < length).astype(jnp.float32)[:, None]
    grad_out = slot_cot.astype(jnp.float32) * valid
    grad_mlp = grad_out.astype(jnp.bfloat16)
    grad_pre = gelu_back(pre, dense_trans(grad_mlp, down_weight)).astype(jnp.bfloat16)
    grad_hidden = grad_out + norm_back(hidden, gain_two, dense_trans(grad_pre, up_weight))
    grad_attended = grad_hidden.astype(jnp.bfloat16)
    grad_inner_out = dense(grad_attended, local_up[:, 3 * RANK :]).astype(jnp.bfloat16)
    up_out_grad = dense_left(grad_attended, inner_out)
    grad_context = (
        dense_trans(grad_attended, out_weight)
        + dense_trans(grad_inner_out, local_down[:, 3 * RANK :])
    ).astype(jnp.bfloat16)
    down_out_grad = dense_left(context_low, grad_inner_out)
    grad_projected = attention_backward(projected, log_total, grad_context).astype(jnp.bfloat16)
    grad_inner = jnp.concatenate(
        [
            dense(
                grad_projected[:, j * width : (j + 1) * width],
                local_up[:, j * RANK : (j + 1) * RANK],
            )
            for j in range(3)
        ],
        axis=1,
    ).astype(jnp.bfloat16)
    up_qkv_grad = jnp.concatenate(
        [
            dense_left(
                grad_projected[:, j * width : (j + 1) * width], inner[:, j * RANK : (j + 1) * RANK]
            )
            for j in range(3)
        ],
        axis=1,
    )
    grad_normed = dense_trans(grad_projected, qkv_weight) + dense_trans(
        grad_inner, local_down[:, : 3 * RANK]
    )
    down_qkv_grad = dense_left(normed, grad_inner)
    grad_input = grad_hidden + norm_back(tokens.astype(jnp.float32), gain_one, grad_normed)
    block_down = jnp.concatenate([down_qkv_grad, down_out_grad], axis=1)
    block_up = jnp.concatenate([up_qkv_grad, up_out_grad], axis=1)
    return (grad_input.astype(jnp.bfloat16), block_down, block_up)


def place_blocks(blocks, slot_ids):
    picks = (slot_ids[:, None] == lax.iota(jnp.int32, ADAPTERS)[None, :]).astype(jnp.float32)
    placed = jnp.einsum("sa,src->rac", picks, blocks, precision=HIGH)
    return placed.reshape(blocks.shape[1], ADAPTERS * blocks.shape[2])


def shards(
    inputs,
    cotangent,
    lengths,
    adapter_ids,
    gain_one,
    gain_two,
    qkv_weight,
    out_weight,
    up_weight,
    down_weight,
    adapter_down,
    adapter_up,
):
    gathered = (
        lax.all_gather(qkv_weight, "shard", axis=0, tiled=True),
        lax.all_gather(out_weight, "shard", axis=0, tiled=True),
        lax.all_gather(up_weight, "shard", axis=0, tiled=True),
        lax.all_gather(down_weight, "shard", axis=0, tiled=True),
        lax.all_gather(adapter_down, "shard", axis=0, tiled=True),
        lax.all_gather(adapter_up, "shard", axis=0, tiled=True),
    )

    def forward_step(carry, slot):
        tokens, length, adapter = slot
        output, saved = forward_slot(tokens, length, adapter, gathered, gain_one, gain_two)
        return (carry, (output, saved))

    outputs_saved = lax.scan(forward_step, None, (inputs, lengths, adapter_ids))[1]
    outputs, saved_all = outputs_saved
    backward_set = (
        lax.all_gather(qkv_weight, "shard", axis=0, tiled=True),
        lax.all_gather(out_weight, "shard", axis=0, tiled=True),
        lax.all_gather(up_weight, "shard", axis=0, tiled=True),
        lax.all_gather(down_weight, "shard", axis=0, tiled=True),
        lax.all_gather(adapter_down, "shard", axis=0, tiled=True),
        lax.all_gather(adapter_up, "shard", axis=0, tiled=True),
    )

    def backward_step(carry, slot):
        tokens, slot_cot, length, adapter, saved = slot
        grad_input, block_down, block_up = backward_slot(
            tokens, slot_cot, length, adapter, saved, backward_set, gain_one, gain_two
        )
        return (carry, (grad_input, block_down, block_up))

    grads, down_blocks, up_blocks = lax.scan(
        backward_step, None, (inputs, cotangent, lengths, adapter_ids, saved_all)
    )[1]
    accum_down = place_blocks(down_blocks, adapter_ids)
    accum_up = place_blocks(up_blocks, adapter_ids)
    owned = (
        lax.psum_scatter(accum_down, "shard", scatter_dimension=0, tiled=True),
        lax.psum_scatter(accum_up, "shard", scatter_dimension=0, tiled=True),
    )
    summed = lax.psum((owned[0], owned[1]), "rep")
    return (outputs, grads, summed[0], summed[1])


def solution(mesh):
    return jax.shard_map(
        shards,
        mesh=mesh,
        in_specs=(
            P(("rep", "shard"), None, None),
            P(("rep", "shard"), None, None),
            P(("rep", "shard")),
            P(("rep", "shard")),
            P(),
            P(),
            P("shard", None),
            P("shard", None),
            P("shard", None),
            P("shard", None),
            P("shard", None),
            P("shard", None),
        ),
        out_specs=(
            P(("rep", "shard"), None, None),
            P(("rep", "shard"), None, None),
            P("shard", None),
            P("shard", None),
        ),
        check_vma=False,
    )
```

profile of v0, /device:TPU:13, one launch (start us, length us, event | category | flops | bytes accessed | tf_op | source)
XLA Modules:
  0.0 857.9 jit_solution(18035500820732537730)
XLA Ops:
  14.1 2.9 copy.42
  18.0 4.0 copy.54
  22.0 1.9 fusion.37
  23.9 24.8 %all-gather.9.cloned.1.call-done = bf16[1024,512]{1,0:T(8,128)(2,1)} async-done(((bf16[128,512]{1,0:T(8,128)(2,1)}), bf16[1024,512]{1,0:T(8,128)(2,1)}) %all-gather.9.cloned.1.call-update) | async-done | bytes 1048592 | tf_op jit(solution)/shard_map/all_gather | solution.py:266
  48.7 2.2 convolution_convert_fusion
  50.9 39.0 %all-gather.11.cloned.1.call-done = bf16[1024,512]{1,0:T(8,128)(2,1)} async-done(((bf16[128,512]{1,0:T(8,128)(2,1)}), bf16[1024,512]{1,0:T(8,128)(2,1)}) %all-gather.11.cloned.1.call-update) | async-done | bytes 1048592 | tf_op jit(solution)/shard_map/all_gather | solution.py:267
  89.9 3.8 fusion.83
  93.7 2.8 fusion.77
  96.5 2.9 fusion.80
  99.4 89.6 %all-gather.7.cloned.1.call-done = bf16[1024,3072]{1,0:T(8,128)(2,1)} async-done(((bf16[128,3072]{1,0:T(8,128)(2,1)}), bf16[1024,3072]{1,0:T(8,128)(2,1)}) %all-gather.7.cloned.1.call-update) | async-done | bytes 6291472 | tf_op jit(solution)/shard_map/all_gather | solution.py:262
  189.0 13.4 %fusion.14 = bf16[1024,3072]{1,0:T(8,128)(2,1)} fusion(f32[1024,1024]{1,0:T(8,128)} %fusion.77, f32[1024,1024]{1,0:T(8,128)} %fusion.80, f32[1024,1024]{1,0:T(8,128)} %fusion.83, bf16[1024,1024]{0,1:T(8,128)(2,1)S(1)} %copy-done.9, bf16[1024,3072]{1,0:T(8,128)(2,1)} %all-gather.7.cloned.1.call-done), kind=kOutput, calls=%fused_computation.29 | convolution fusion | flops 6455033856 | bytes 27262976 | tf_op jit(solution)/shard_map/while/body/eval_jaxpr/dot_general | solution.py:40
  202.3 4.5 fusion.134
  206.9 1.0 copy-done.22
  207.9 2.4 fusion.135
  210.4 2.9 copy.52
  213.2 3.0 copy.48
  216.3 2.3 copy.51
  218.6 2.7 copy.47
  221.3 10.0 %select_reduce_fusion.1 = (f32[16,512]{1,0:T(8,128)S(1)}, f32[16,512,512]{1,2,0:T(8,128)}) fusion(pred[512,512]{0,1:T(8,128)(4,1)S(1)} %iota_compare_fusion.1, bf16[512,16,64]{0,2,1:T(8,128)(2,1)} %bitcast.155, bf16[512,16,64]{0,2,1:T(8,128)(2,1)} %bitcast.151), kind=kOutput, calls=%fused_computation.26 | convolution fusion | flops 549445632 | bytes 19169280 | tf_op jit(solution)/shard_map/while/body/eval_jaxpr/qhd,khd->hqk/dot_general | solution.py:68
  231.3 13.8 %select_reduce_fusion = (f32[16,512]{1,0:T(8,128)S(1)}, f32[16,512,1024]{2,1,0:T(8,128)}) fusion(pred[512,1024]{1,0:T(8,128)(4,1)S(1)} %iota_compare_fusion, bf16[512,16,64]{0,2,1:T(8,128)(2,1)S(1)} %bitcast.146, bf16[1024,16,64]{0,2,1:T(8,128)(2,1)S(1)} %bitcast.138), kind=kOutput, calls=%fused_computation.5 | convolution fusion | flops 1098899456 | bytes 37257216 | tf_op jit(solution)/shard_map/while/body/eval_jaxpr/qhd,khd->hqk/dot_general | solution.py:68
  245.1 9.7 %fusion.13 = f32[16,512]{1,0:T(8,128)S(1)} fusion(f32[16,512,512]{1,2,0:T(8,128)} %get-tuple-element.248, f32[16,512]{1,0:T(8,128)S(1)} %get-tuple-element.247, pred[512,512]{0,1:T(8,128)(4,1)S(1)} %iota_compare_fusion.1), kind=kLoop, calls=%fused_computation.27 | loop fusion | flops 16769024 | bytes 17104896 | tf_op jit(solution)/shard_map/while/body/eval_jaxpr/reduce_sum | solution.py:89
  254.8 1.4 copy.46
  256.2 2.9 copy.50
  259.1 15.8 %fusion = f32[16,512]{1,0:T(8,128)S(1)} fusion(f32[16,512,1024]{2,1,0:T(8,128)} %get-tuple-element.246, f32[16,512]{1,0:T(8,128)S(1)} %get-tuple-element.245, pred[512,1024]{1,0:T(8,128)(4,1)S(1)} %iota_compare_fusion), kind=kLoop, calls=%fused_computation.6 | loop fusion | flops 33546240 | bytes 34144256 | tf_op jit(solution)/shard_map/while/body/eval_jaxpr/reduce_sum | solution.py:89
  274.8 8.6 %fusion.71 = bf16[512,16,64]{0,2,1:T(8,128)(2,1)S(1)} fusion(bf16[512,16,64]{0,2,1:T(8,128)(2,1)S(1)} %bitcast.162, f32[16,512,512]{1,2,0:T(8,128)} %get-tuple-element.248, f32[16,512]{1,0:T(8,128)S(1)} %fusion.13, f32[16,512]{1,0:T(8,128)S(1)} %get-tuple-element.247, pred[512,512]{0,1:T(8,128)(4,1)S(1)} %iota_compare_fusion.1), kind=kOutput, calls=%fused_computation.93 | convolution fusion | flops 558366720 | bytes 19202048 | tf_op jit(solution)/shard_map/while/body/eval_jaxpr/hqk,khd->qhd/dot_general | solution.py:92
  283.5 15.0 %fusion.70 = bf16[512,16,64]{0,2,1:T(8,128)(2,1)S(1)} fusion(bf16[1024,16,64]{0,2,1:T(8,128)(2,1)S(1)} %bitcast.153, f32[16,512,1024]{2,1,0:T(8,128)} %get-tuple-element.246, f32[16,512]{1,0:T(8,128)S(1)} %fusion, f32[16,512]{1,0:T(8,128)S(1)} %get-tuple-element.245, pred[512,1024]{1,0:T(8,128)(4,1)S(1)} %iota_compare_fusion), kind=kOutput, calls=%fused_computation.92 | convolution fusion | flops 1116209152 | bytes 37289984 | tf_op jit(solution)/shard_map/while/body/eval_jaxpr/hqk,khd->qhd/dot_general | solution.py:92
  298.7 1.3 copy-done.12
  300.0 1.4 convolution_convert_fusion.5
  301.5 4.8 fusion.140
  306.4 1.8 fusion.137
  308.2 1.9 copy-done.3
  310.7 52.6 %all-gather.15.cloned.1.call-done = bf16[1024,4096]{1,0:T(8,128)(2,1)} async-done(((bf16[128,4096]{1,0:T(8,128)(2,1)}), bf16[1024,4096]{1,0:T(8,128)(2,1)}) %all-gather.15.cloned.1.call-update) | async-done | bytes 8388624 | tf_op jit(solution)/shard_map/all_gather | solution.py:264
  363.3 17.0 %fusion.46 = f32[1024,4096]{1,0:T(8,128)} fusion(bf16[1024,4096]{1,0:T(8,128)(2,1)} %all-gather.15.cloned.1.call-done, f32[1024,1024]{0,1:T(8,128)} %copy-done.3, f32[1024]{0:T(1024)S(1)} %copy-done.48, f32[1024]{0:T(1024)S(1)} %fusion.99, f32[1024]{0:T(1024)S(1)} %broadcast_multiply_fusion.2), kind=kOutput, calls=%fused_computation.71 | convolution fusion | flops 8594128896 | bytes 29372416 | tf_op jit(solution)/shard_map/while/body/eval_jaxpr/dot_general | solution.py:40
  380.3 107.7 %all-gather.17.cloned.1.call-done = bf16[4096,1024]{1,0:T(8,128)(2,1)} async-done(((bf16[512,1024]{1,0:T(8,128)(2,1)}), bf16[4096,1024]{1,0:T(8,128)(2,1)}) %all-gather.17.cloned.1.call-update) | async-done | bytes 8388624 | tf_op jit(solution)/shard_map/all_gather | solution.py:265
  488.0 29.5 %multiply_reduce_fusion.2 = (f32[1024]{0:T(1024)S(1)}, f32[1024,1024]{0,1:T(8,128)}) fusion(f32[1024,1024]{0,1:T(8,128)} %copy-done.3, f32[1024]{0:T(1024)S(1)} %copy-done.48, f32[1024]{0:T(1024)S(1)} %broadcast_multiply_fusion.2, bf16[1024,4096]{1,0:T(8,128)(2,1)} %all-gather.15.cloned.1.call-done, f32[1024,4096]{1,0:T(8,128)} %fusion.46, ...), kind=kOutput, calls=%fused_computation.66 | convolution fusion | flops 17271095296 | bytes 44056576 | tf_op jit(solution)/shard_map/while/body/eval_jaxpr/dot_general | solution.py:44
  517.5 4.5 fusion.133
  524.7 1.8 convolution_convert_fusion.4
  527.2 2.3 fusion.143
  529.5 1.9 add_convert_fusion.1
  531.4 1.5 fusion.136
  532.9 5.6 fusion.63
  538.5 12.2 %multiply_reduce_fusion.1 = (f32[16,512]{1,0:T(8,128)S(1)}, f32[16,512,512]{1,2,0:T(8,128)}) fusion(f32[16,512,512]{1,2,0:T(8,128)} %get-tuple-element.248, f32[16,512]{1,0:T(8,128)S(1)} %log_add_fusion.1, pred[512,512]{0,1:T(8,128)(4,1)S(1)} %copy-done.27, bf16[512,16,64]{0,2,1:T(8,128)(2,1)} %bitcast.164, bf16[512,16,64]{0,2,1:T(8,128)(2,1)} %bitcast.161), kind=kOutput, calls=%fused_computation.18 | convolution fusion | flops 557834240 | bytes 35979264 | tf_op jit(solution)/shard_map/while/body/eval_jaxpr/qhd,khd->hqk/dot_general | solution.py:121
  550.7 12.4 %multiply_convert_fusion.1 = bf16[16,512,512]{1,2,0:T(8,128)(2,1)S(1)} fusion(f32[16,512,512]{1,2,0:T(8,128)} %get-tuple-element.254, f32[16,512,512]{1,2,0:T(8,128)} %get-tuple-element.248, f32[16,512]{1,0:T(8,128)S(1)} %get-tuple-element.253, f32[16,512]{1,0:T(8,128)S(1)} %log_add_fusion.1, pred[512,512]{0,1:T(8,128)(4,1)S(1)} %copy-done.27), kind=kLoop, calls=%fused_computation.17 | loop fusion | flops 25165824 | bytes 42270720 | tf_op jit(solution)/shard_map/while/body/eval_jaxpr/convert_element_type | solution.py:126
  563.2 2.5 fusion.68
  565.6 4.0 multiply_bitcast_fusion
  569.6 25.8 %multiply_reduce_fusion = (f32[16,512]{1,0:T(8,128)S(1)}, f32[16,512,1024]{2,1,0:T(8,128)}) fusion(f32[16,512,1024]{2,1,0:T(8,128)} %get-tuple-element.246, f32[16,512]{1,0:T(8,128)S(1)} %log_add_fusion, pred[512,1024]{1,0:T(8,128)(4,1)S(1)} %iota_compare_fusion, bf16[512,16,64]{0,2,1:T(8,128)(2,1)S(1)} %bitcast.160, bf16[1024,16,64]{0,2,1:T(8,128)(2,1)S(1)} %bitcast.154), kind=kOutput, calls=%fused_computation.1 | convolution fusion | flops 1115676672 | bytes 70844416 | tf_op jit(solution)/shard_map/while/body/eval_jaxpr/qhd,khd->hqk/dot_general | solution.py:121
  595.4 15.3 %fusion.41 = bf16[1024,16,64]{0,2,1:T(8,128)(2,1)S(1)} fusion(f32[512,16,64]{0,2,1:T(8,128)} %fusion.63, bf16[512,16,64]{0,2,1:T(8,128)(2,1)} %bitcast.159, f32[16,512,1024]{2,1,0:T(8,128)} %get-tuple-element.246, f32[16,512]{1,0:T(8,128)S(1)} %log_add_fusion, pred[512,1024]{1,0:T(8,128)(4,1)S(1)} %iota_compare_fusion), kind=kOutput, calls=%fused_computation.60 | convolution fusion | flops 1109393408 | bytes 39354368 | tf_op jit(solution)/shard_map/while/body/eval_jaxpr/hqk,qhd->khd/dot_general | solution.py:119
  612.1 28.0 %multiply_convert_fusion = bf16[16,512,1024]{2,1,0:T(8,128)(2,1)} fusion(f32[16,512,1024]{2,1,0:T(8,128)} %get-tuple-element.256, f32[16,512,1024]{2,1,0:T(8,128)} %get-tuple-element.246, f32[16,512]{1,0:T(8,128)S(1)} %get-tuple-element.255, f32[16,512]{1,0:T(8,128)S(1)} %log_add_fusion, pred[512,1024]{1,0:T(8,128)(4,1)S(1)} %iota_compare_fusion), kind=kLoop, calls=%fused_computation | loop fusion | flops 50331648 | bytes 84475904 | tf_op jit(solution)/shard_map/while/body/eval_jaxpr/convert_element_type | solution.py:126
  640.1 12.1 %fusion.69 = bf16[512,16,64]{0,2,1:T(8,128)(2,1)} fusion(bf16[1024,16,64]{0,2,1:T(8,128)(2,1)S(1)} %bitcast.139, bf16[16,512,1024]{2,1,0:T(8,128)(2,1)} %multiply_convert_fusion), kind=kOutput, calls=%fused_computation.91 | convolution fusion | flops 1074790400 | bytes 19922944 | tf_op jit(solution)/shard_map/while/body/eval_jaxpr/hqk,khd->qhd/dot_general | solution.py:128
  652.1 9.5 %fusion.42 = bf16[1024,16,64]{0,2,1:T(8,128)(2,1)S(1)} fusion(f32[512,16,64]{0,2,1:T(8,128)} %multiply_bitcast_fusion, bf16[512,16,64]{0,2,1:T(8,128)(2,1)S(1)} %bitcast.147, bf16[16,512,1024]{2,1,0:T(8,128)(2,1)} %multiply_convert_fusion), kind=kOutput, calls=%fused_computation.62 | convolution fusion | flops 1076887552 | bytes 22020096 | tf_op jit(solution)/shard_map/while/body/eval_jaxpr/hqk,qhd->khd/dot_general | solution.py:134
  663.3 1.5 copy-done.18
  668.0 2.6 broadcast_multiply_fusion
  671.4 11.0 %fusion.23 = f32[1024,1024]{0,1:T(8,128)S(1)} fusion(bf16[1024,3072]{1,0:T(8,128)(2,1)} %all-gather.7.cloned.1.call-done, bf16[1024,1024]{0,1:T(8,128)(2,1)} %bitcast.149, bf16[1024,1024]{0,1:T(8,128)(2,1)} %bitcast.137, bf16[1024,1024]{0,1:T(8,128)(2,1)} %bitcast.142), kind=kOutput, calls=%fused_computation.36 | convolution fusion | flops 6461325312 | bytes 16777216 | tf_op jit(solution)/shard_map/while/body/eval_jaxpr/dot_general | solution.py:44
  682.5 2.1 fusion.38
  684.6 1.9 copy-done.5
  687.6 16.9 %fusion.47 = bf16[1,1024,1024]{1,2,0:T(8,128)(2,1)} fusion(f32[1024,1024]{0,1:T(8,128)} %copy-done.3, f32[1024]{0:T(1024)S(1)} %copy-done.43, bf16[4096,1024]{1,0:T(8,128)(2,1)} %all-gather.17.cloned.1.call-done, f32[1024,4096]{1,0:T(8,128)} %fusion.46), kind=kOutput, calls=%fused_computation.72 | convolution fusion | flops 8630829056 | bytes 31461376 | tf_op jit(solution)/shard_map/while/body/eval_jaxpr/dot_general | solution.py:40
  704.5 35.0 %reduce-scatter.3.cloned.1.call-done = f32[128,512]{0,1:T(8,128)} async-done(((f32[1024,512]{0,1:T(8,128)}), f32[128,512]{0,1:T(8,128)}) %reduce-scatter.3.cloned.1.call-update) | async-done | bytes 262160 | tf_op jit(solution)/shard_map/reduce_scatter | solution.py:299
  739.5 71.8 %reduce-scatter.5.cloned.1.call-done = f32[128,512]{0,1:T(8,128)} async-done(((f32[1024,512]{0,1:T(8,128)}), f32[128,512]{0,1:T(8,128)}) %reduce-scatter.5.cloned.1.call-update) | async-done | bytes 262160 | tf_op jit(solution)/shard_map/reduce_scatter | solution.py:300
  811.3 7.2 fusion.48
  818.5 4.1 copy.58
  822.6 2.5 copy.59
  825.2 22.2 %all-reduce.5.cloned.1.call-done = (f32[128,512]{0,1:T(8,128)}, f32[128,512]{0,1:T(8,128)}) async-done(((f32[128,512]{0,1:T(8,128)}, f32[128,512]{0,1:T(8,128)}), (f32[128,512]{0,1:T(8,128)}, f32[128,512]{0,1:T(8,128)})) %all-reduce.5.cloned.1.call-update) | async-done | bytes 524304 | tf_op jit(solution)/shard_map/psum | solution.py:302
  847.4 1.8 copy.60
  849.2 1.8 copy.61
  (157 shorter events, 18.5 us)
Async XLA Ops:
  7.2 41.6 %all-gather.9.cloned.1.call-start = ((), (), s32[]{:S(2)}) async-start(), calls=%async_computation.3 | async-start | bytes 1179648 | tf_op jit(solution)/shard_map/all_gather | solution.py:266
  7.9 82.0 %all-gather.11.cloned.1.call-start = ((), (), s32[]{:S(2)}) async-start(), calls=%async_computation.4 | async-start | bytes 1179648 | tf_op jit(solution)/shard_map/all_gather | solution.py:267
  8.6 180.3 %all-gather.7.cloned.1.call-start = ((), (), s32[]{:S(2)}) async-start(), calls=%async_computation.2 | async-start | bytes 7077888 | tf_op jit(solution)/shard_map/all_gather | solution.py:262
  9.4 292.1 %all-gather.13.cloned.1.call-start = ((), (), s32[]{:S(2)}) async-start(), calls=%async_computation.5 | async-start | bytes 2359296 | tf_op jit(solution)/shard_map/all_gather | solution.py:263
  10.0 353.3 %all-gather.15.cloned.1.call-start = ((), (), s32[]{:S(2)}) async-start(), calls=%async_computation.6 | async-start | bytes 9437184 | tf_op jit(solution)/shard_map/all_gather | solution.py:264
  10.5 477.4 %all-gather.17.cloned.1.call-start = ((), (), s32[]{:S(2)}) async-start(), calls=%async_computation.7 | async-start | bytes 9437184 | tf_op jit(solution)/shard_map/all_gather | solution.py:265
  11.1 728.4 %reduce-scatter.3.cloned.1.call-start = ((), (), s32[]{:S(2)}) async-start(), calls=%async_computation.8 | async-start | bytes 2359296 | tf_op jit(solution)/shard_map/reduce_scatter | solution.py:299
  11.3 263.6 %copy-start.26 = (pred[512,512]{0,1:T(8,128)(4,1)}, pred[512,512]{0,1:T(8,128)(4,1)S(1)}, u32[]{:S(2)}) copy-start(pred[512,512]{0,1:T(8,128)(4,1)S(1)} %iota_compare_fusion.1) | copy-start | bytes 786436
  16.9 5.0 copy-start
  17.0 5.0 copy-start.46
  17.3 6.6 copy-start.36
  18.0 6.0 copy-start.40
  18.0 5.9 copy-start.38
  50.9 45.6 %copy-start.34 = (bf16[1024,48]{0,1:T(8,128)(2,1)}, bf16[1024,48]{0,1:T(8,128)(2,1)S(1)}, u32[]{:S(2)}) copy-start(bf16[1024,48]{0,1:T(8,128)(2,1)S(1)} %convolution_convert_fusion) | copy-start | bytes 294916
  89.9 3.8 copy-start.29
  93.7 95.3 %copy-start.9 = (bf16[1024,1024]{0,1:T(8,128)(2,1)S(1)}, bf16[1024,1024]{0,1:T(8,128)(2,1)}, u32[]{:S(2)}) copy-start(bf16[1024,1024]{0,1:T(8,128)(2,1)} %fusion.37) | copy-start | bytes 6291460
  202.3 5.6 copy-start.22
  213.2 18.1 %copy-start.7 = (bf16[1024,1024]{0,1:T(8,128)(2,1)}, bf16[1024,1024]{0,1:T(8,128)(2,1)S(1)}, u32[]{:S(2)}) copy-start(bf16[1024,1024]{0,1:T(8,128)(2,1)S(1)} %copy.52) | copy-start | bytes 6291460
  221.3 10.0 %copy-start.14 = (bf16[512,1024]{0,1:T(8,128)(2,1)S(1)}, bf16[512,1024]{0,1:T(8,128)(2,1)}, u32[]{:S(2)}) copy-start(bf16[512,1024]{0,1:T(8,128)(2,1)} %copy.51) | copy-start | bytes 3145732
  245.1 9.7 %copy-start.33 = (bf16[512,1024]{1,0:T(8,128)(2,1)S(1)}, bf16[512,1024]{1,0:T(8,128)(2,1)}, u32[]{:S(2)}) copy-start(bf16[512,1024]{1,0:T(8,128)(2,1)} %get-tuple-element.238) | copy-start | bytes 3145732
  259.0 24.4 %copy-start.20 = (bf16[1024,1024]{0,1:T(8,128)(2,1)}, bf16[1024,1024]{0,1:T(8,128)(2,1)S(1)}, u32[]{:S(2)}) copy-start(bf16[1024,1024]{0,1:T(8,128)(2,1)S(1)} %copy.50) | copy-start | bytes 6291460
  259.0 15.8 %copy-start.31 = (bf16[512,1024]{0,1:T(8,128)(2,1)S(1)}, bf16[512,1024]{0,1:T(8,128)(2,1)}, u32[]{:S(2)}) copy-start(bf16[512,1024]{0,1:T(8,128)(2,1)} %copy.46) | copy-start | bytes 3145732
  298.7 1.3 copy-start.12
  301.5 4.9 copy-start.1
  308.2 2.0 copy-start.3
  308.2 55.1 %copy-start.48 = (f32[1024]{0:T(1024)S(1)}, f32[1024]{0:T(1024)}, u32[]{:S(2)}) copy-start(f32[1024]{0:T(1024)} %param.29) | copy-start | bytes 12292
  310.7 177.3 %copy-start.16 = (bf16[1,1024,1024]{1,2,0:T(8,128)(2,1)S(1)}, bf16[1,1024,1024]{1,2,0:T(8,128)(2,1)}, u32[]{:S(2)}) copy-start(bf16[1,1024,1024]{1,2,0:T(8,128)(2,1)} %copy.54) | copy-start | bytes 6291460
  310.7 177.2 %copy-start.42 = (f32[1024]{0:T(1024)S(1)}, f32[1024]{0:T(1024)}, u32[]{:S(2)}) copy-start(f32[1024]{0:T(1024)} %fusion.97) | copy-start | bytes 12292
  522.1 2.0 copy-start.4
  522.1 2.0 copy-start.44
  524.1 2.4 copy-start.13
  524.1 3.1 copy-start.50
  524.7 8.2 slice-start
  527.1 5.8 slice-start.1
  527.1 5.8 slice-start.2
  529.5 3.4 slice-start.3
  529.5 3.4 copy-start.27
  550.7 12.4 %copy-start.19 = (bf16[512,1024]{0,1:T(8,128)(2,1)S(1)}, bf16[512,1024]{0,1:T(8,128)(2,1)}, u32[]{:S(2)}) copy-start(bf16[512,1024]{0,1:T(8,128)(2,1)} %copy.48) | copy-start | bytes 3145732
  563.1 2.5 copy-start.23
  565.6 4.0 copy-start.21
  565.6 4.0 copy-start.28
  595.4 15.3 %copy-start.35 = (bf16[1024,48]{0,1:T(8,128)(2,1)S(1)}, bf16[1024,48]{0,1:T(8,128)(2,1)}, u32[]{:S(2)}) copy-start(bf16[1024,48]{0,1:T(8,128)(2,1)} %copy-done.34) | copy-start | bytes 294916
  610.7 1.3 copy-start.17
  612.1 28.0 %copy-start.8 = (bf16[1024,1024]{0,1:T(8,128)(2,1)S(1)}, bf16[1024,1024]{0,1:T(8,128)(2,1)}, u32[]{:S(2)}) copy-start(bf16[1024,1024]{0,1:T(8,128)(2,1)} %copy-done.7) | copy-start | bytes 6291460
  640.0 12.1 %copy-start.15 = (bf16[512,1024]{0,1:T(8,128)(2,1)S(1)}, bf16[512,1024]{0,1:T(8,128)(2,1)}, u32[]{:S(2)}) copy-start(bf16[512,1024]{0,1:T(8,128)(2,1)} %copy.51) | copy-start | bytes 3145732
  652.1 10.2 %copy-start.25 = (bf16[512,16,64]{0,2,1:T(8,128)(2,1)S(1)}, bf16[512,16,64]{0,2,1:T(8,128)(2,1)}, u32[]{:S(2)}) copy-start(bf16[512,16,64]{0,2,1:T(8,128)(2,1)} %fusion.68) | copy-start | bytes 3145732
  652.1 10.2 %copy-start.32 = (bf16[512,16,64]{0,2,1:T(8,128)(2,1)S(1)}, bf16[512,16,64]{0,2,1:T(8,128)(2,1)}, u32[]{:S(2)}) copy-start(bf16[512,16,64]{0,2,1:T(8,128)(2,1)} %fusion.69) | copy-start | bytes 3145732
  661.7 3.9 copy-start.6
  661.7 3.1 copy-start.18
  661.7 3.4 copy-start.30
  662.6 3.4 copy-start.11
  665.6 1.6 copy-start.10
  666.1 1.9 copy-start.49
  670.6 140.7 %reduce-scatter.5.cloned.1.call-start = ((), (), s32[]{:S(2)}) async-start(), calls=%async_computation.9 | async-start | bytes 2359296 | tf_op jit(solution)/shard_map/reduce_scatter | solution.py:300
  671.3 11.1 %copy-start.2 = (bf16[1,1024,1024]{1,2,0:T(8,128)(2,1)S(1)}, bf16[1,1024,1024]{1,2,0:T(8,128)(2,1)}, u32[]{:S(2)}) copy-start(bf16[1,1024,1024]{1,2,0:T(8,128)(2,1)} %copy-done) | copy-start | bytes 6291460
  671.3 11.1 %copy-start.37 = (f32[1024]{0:T(1024)S(1)}, f32[1024]{0:T(1024)}, u32[]{:S(2)}) copy-start(f32[1024]{0:T(1024)} %copy-done.36) | copy-start | bytes 12292
  671.3 11.1 %copy-start.47 = (f32[1024]{0:T(1024)S(1)}, f32[1024]{0:T(1024)}, u32[]{:S(2)}) copy-start(f32[1024]{0:T(1024)} %param.28) | copy-start | bytes 12292
  671.3 176.0 %all-reduce.5.cloned.1.call-start = ((), (), s32[]{:S(2)}) async-start(), calls=%async_computation.10 | async-start | bytes 1048576 | tf_op jit(solution)/shard_map/psum | solution.py:302
  682.5 2.1 copy-start.41
  682.5 4.1 copy-start.39
  684.5 2.0 copy-start.5
  684.6 3.0 copy-start.43
  687.5 123.8 %copy-start.45 = (f32[1024]{0:T(1024)S(1)}, f32[1024]{0:T(1024)}, u32[]{:S(2)}) copy-start(f32[1024]{0:T(1024)} %copy-done.44) | copy-start | bytes 12292
  818.5 4.1 copy-start.24
Sparse Core Ops, SparseCore 0:
  10.1 38.5 all-gather.8
  50.9 38.9 all-gather.10
  92.1 96.8 all-gather.6
  190.9 48.6 all-gather.12
  241.6 121.6 all-gather.14
  365.3 122.6 all-gather.16
  670.7 68.7 reduce-scatter.2
  743.0 68.1 reduce-scatter.4
  813.7 33.6 all-reduce.4
where the time goes:
time: 869 us; the launch traced here: 858 us
  waiting for transfers between devices  447 us (51%)
  matrix products  255 us (29%)
  other arithmetic  87.7 us (10%)
  local copies, waits for them, and re-layouts  51.1 us (6%)
  between operations  16.3 us (2%)
    all_gather x1, waiting for transfers between devices, shards(): lax.all_gather(down_weight, 'shard', axis=0, tiled=True)  108 us
    all_gather x1, waiting for transfers between devices, shards(): lax.all_gather(qkv_weight, 'shard', axis=0, tiled=True)  89.6 us
    reduce_scatter x1, waiting for transfers between devices, shards(): lax.psum_scatter(accum_up, 'shard', scatter_dimension=0, tiled=True)  71.8 us
    dot_general x10, matrix products, dense(): return jnp.dot(left, right, preferred_element_type=jnp.float32)  59 us
    dot_general x9, matrix products, dense_trans(): lax.dot_general(left, right, (((1,), (1,)), ((), ())), preferred_element_...  58.1 us
    all_gather x1, waiting for transfers between devices, shards(): lax.all_gather(up_weight, 'shard', axis=0, tiled=True)  52.6 us
    convert_element_type x2, other arithmetic, attention_backward(): grad_scores = (probs * (grad_probs - jnp.sum(probs * grad_probs, axis=-1,...  40.4 us
    all_gather x1, waiting for transfers between devices, shards(): lax.all_gather(adapter_up, 'shard', axis=0, tiled=True)  39 us
  transfers between devices with their start and end apart: 9, of which 8 were waited for; matrix products, arithmetic and copies ran while one was open for 24% of the time, Pallas kernels for 0%

commit v1 on v0

--- a/solution.py
+++ b/solution.py
@@ -1,7 +1,12 @@
+import functools
+
 import jax
 import jax.numpy as jnp
 from jax import lax
+from jax.experimental import pallas as pl
+from jax.experimental.pallas import tpu as pltpu
 from jax.sharding import PartitionSpec as P
+
 
 HEADS = 16
 RANK = 16
@@ -244,6 +249,139 @@
     return placed.reshape(blocks.shape[1], ADAPTERS * blocks.shape[2])
 
 
+MESH = pl.DeviceIdType.MESH
+
+def mesh_split(n_rep, n_shard):
+    zs = 4 if n_shard % 4 == 0 else n_shard
+    return zs, n_shard // zs
+
+def share_rows(rows):
+    return max(16, rows * 3 // 8 // 16 * 16)
+
+def chunk_list(shapes, width):
+    out = []
+    for w, (rows, cols) in enumerate(shapes):
+        for r0 in range(0, rows, 128):
+            for c0 in range(0, cols, width):
+                out.append((w, r0, min(rows, 128), c0, min(width, cols)))
+    return out
+
+def gather_kernel(n_w, zs, ys, chunks, *refs):
+    ins = refs[:n_w]
+    outs = refs[n_w:2 * n_w]
+    zsend, zrecv, ysend, yrecv, xsend, xrecv, csend, crecv, lsem = refs[2 * n_w:]
+    r = lax.axis_index("rep")
+    s = lax.axis_index("shard")
+    z, y = s // ys, lax.rem(s, ys)
+    core = lax.rem(r, 2)
+    xp = lax.rem(r // 2, 2)
+    sib = r + 1 - 2 * core
+    par = r + 2 - 4 * xp
+    zpeers = [lax.rem(z + k, zs) for k in range(1, zs)]
+    ypeers = [lax.rem(y + k, ys) for k in range(1, ys)]
+    peers = [(r, zz * ys + y) for zz in zpeers] + [(r, z * ys + yy) for yy in ypeers] + [(par, s), (sib, s)]
+    local = []
+    for w in range(n_w):
+        cp = pltpu.make_async_copy(ins[w], outs[w].at[z, y], lsem.at[w])
+        cp.start()
+        local.append(cp)
+    bar = pltpu.get_barrier_semaphore()
+    for p in peers:
+        pl.semaphore_signal(bar, inc=1, device_id=p, device_id_type=MESH)
+    pl.semaphore_wait(bar, len(peers))
+
+    def rdma(src, dst, ss, rs, dev):
+        cp = pltpu.make_async_remote_copy(src_ref=src, dst_ref=dst, send_sem=ss, recv_sem=rs, device_id=dev, device_id_type=MESH)
+        cp.start()
+
+    def geom(t):
+        w, r0, rows, c0, cols = chunks[t]
+        a = share_rows(rows)
+        half = cols // 2
+        mine = pl.ds(pl.multiple_of(r0 + xp * a, 16), rows - a)
+        excl = pl.ds(pl.multiple_of(r0 + xp * (rows - a), 16), a)
+        missing = pl.ds(pl.multiple_of(r0 + (1 - xp) * (rows - a), 16), a)
+        col = pl.ds(pl.multiple_of(c0 + core * half, 128), half)
+        return w, a, half, rows, mine, excl, missing, col
+
+    def wait_total(elems, sem):
+        for out in outs:
+            _, _, big_r, big_n = out.shape
+            for lead in range(1, zs + 1):
+                for take in range(big_r, 0, -16):
+                    if elems % (lead * take * 128) == 0 and elems // (lead * take) <= big_n:
+                        reg = out.at[pl.ds(0, lead), 0, pl.ds(0, take), pl.ds(0, elems // (lead * take))]
+                        pltpu.make_async_copy(reg, reg, sem).wait()
+                        return
+        raise ValueError("no region")
+
+    def stage_z(t):
+        w, a, half, rows, mine, excl, missing, col = geom(t)
+        for zz in zpeers:
+            rdma(ins[w].at[mine, col], outs[w].at[z, y, mine, col], zsend.at[t], zrecv.at[t], (r, zz * ys + y))
+
+    def stage_y(t):
+        w, a, half, rows, mine, excl, missing, col = geom(t)
+        wait_total((zs - 1) * (rows - a) * half, zrecv.at[t])
+        for yy in ypeers:
+            rdma(outs[w].at[:, y, mine, col], outs[w].at[:, y, mine, col], ysend.at[t], yrecv.at[t], (r, z * ys + yy))
+        for zz in zpeers:
+            rdma(outs[w].at[zz, y, excl, col], outs[w].at[zz, y, excl, col], xsend.at[t], xrecv.at[t], (par, s))
+            rdma(outs[w].at[zz, y, mine, col], outs[w].at[zz, y, mine, col], csend.at[t], crecv.at[t], (sib, s))
+
+    def stage_x(t):
+        w, a, half, rows, mine, excl, missing, col = geom(t)
+        wait_total((ys - 1) * zs * (rows - a) * half, yrecv.at[t])
+        for yy in ypeers:
+            rdma(outs[w].at[:, yy, excl, col], outs[w].at[:, yy, excl, col], xsend.at[t], xrecv.at[t], (par, s))
+            rdma(outs[w].at[:, yy, mine, col], outs[w].at[:, yy, mine, col], csend.at[t], crecv.at[t], (sib, s))
+
+    def stage_c(t):
+        w, a, half, rows, mine, excl, missing, col = geom(t)
+        wait_total((zs * ys - 1) * a * half, xrecv.at[t])
+        for zz in zpeers:
+            rdma(outs[w].at[zz, y, missing, col], outs[w].at[zz, y, missing, col], csend.at[t], crecv.at[t], (sib, s))
+        for yy in ypeers:
+            rdma(outs[w].at[:, yy, missing, col], outs[w].at[:, yy, missing, col], csend.at[t], crecv.at[t], (sib, s))
+
+    n = len(chunks)
+    for t in range(n):
+        stage_z(t)
+    for cp in local:
+        cp.wait()
+    for t in range(n + 2):
+        if t < n:
+            stage_y(t)
+        if 0 <= t - 1 < n:
+            stage_x(t - 1)
+        if 0 <= t - 2 < n:
+            stage_c(t - 2)
+    for t in range(n):
+        w, a, half, rows, mine, excl, missing, col = geom(t)
+        wait_total((zs * ys - 1) * rows * half, crecv.at[t])
+        wait_total((zs * ys - 1) * rows * half, csend.at[t])
+        wait_total((zs * ys - 1) * a * half, xsend.at[t])
+        wait_total((zs - 1) * (rows - a) * half, zsend.at[t])
+        wait_total((ys - 1) * zs * (rows - a) * half, ysend.at[t])
+
+
+def gather_all(shards, n_rep, n_shard, width=1024, cid=0):
+    zs, ys = mesh_split(n_rep, n_shard)
+    chunks = chunk_list([w.shape for w in shards], width)
+    n = len(chunks)
+    nw = len(shards)
+    res = pl.pallas_call(
+        functools.partial(gather_kernel, nw, zs, ys, chunks),
+        out_shape=[jax.ShapeDtypeStruct((zs, ys) + w.shape, w.dtype) for w in shards],
+        in_specs=[pl.BlockSpec(memory_space=pltpu.VMEM)] * nw,
+        out_specs=[pl.BlockSpec(memory_space=pl.ANY)] * nw,
+        scratch_shapes=[pltpu.SemaphoreType.DMA((n,))] * 8 + [pltpu.SemaphoreType.DMA((nw,))],
+        compiler_params=pltpu.CompilerParams(collective_id=cid, has_side_effects=True),
+        name="gather_weights",
+    )(*shards)
+    return [v.reshape((-1, v.shape[-1])) for v in res]
+
+
 def shards(
     inputs,
     cotangent,
@@ -258,13 +396,10 @@
     adapter_down,
     adapter_up,
 ):
-    gathered = (
-        lax.all_gather(qkv_weight, "shard", axis=0, tiled=True),
-        lax.all_gather(out_weight, "shard", axis=0, tiled=True),
-        lax.all_gather(up_weight, "shard", axis=0, tiled=True),
-        lax.all_gather(down_weight, "shard", axis=0, tiled=True),
-        lax.all_gather(adapter_down, "shard", axis=0, tiled=True),
-        lax.all_gather(adapter_up, "shard", axis=0, tiled=True),
+    gathered = gather_all(
+        (qkv_weight, out_weight, up_weight, down_weight, adapter_down, adapter_up),
+        lax.axis_size("rep"),
+        lax.axis_size("shard"),
     )
 
     def forward_step(carry, slot):
@@ -274,19 +409,10 @@
 
     outputs_saved = lax.scan(forward_step, None, (inputs, lengths, adapter_ids))[1]
     outputs, saved_all = outputs_saved
-    backward_set = (
-        lax.all_gather(qkv_weight, "shard", axis=0, tiled=True),
-        lax.all_gather(out_weight, "shard", axis=0, tiled=True),
-        lax.all_gather(up_weight, "shard", axis=0, tiled=True),
-        lax.all_gather(down_weight, "shard", axis=0, tiled=True),
-        lax.all_gather(adapter_down, "shard", axis=0, tiled=True),
-        lax.all_gather(adapter_up, "shard", axis=0, tiled=True),
-    )
-
     def backward_step(carry, slot):
         tokens, slot_cot, length, adapter, saved = slot
         grad_input, block_down, block_up = backward_slot(
-            tokens, slot_cot, length, adapter, saved, backward_set, gain_one, gain_two
+            tokens, slot_cot, length, adapter, saved, gathered, gain_one, gain_two
         )
         return (carry, (grad_input, block_down, block_up))
 

time: 869 us -> 678 us (0.78)
  waiting for transfers between devices: 447 us -> 127 us
  Pallas kernels: 0 us -> 137 us
    all_gather x6 -> x0, waiting for transfers between devices: 314 us -> none  [the longest x1 108 us: shards(): lax.all_gather(down_weight, 'shard', axis=0, tiled=True)]
    pallas_call x0 -> x1, Pallas kernels: none -> 137 us  [gather_all(): pl.pallas_call(functools.partial(gather_kernel, nw, zs, ys, chunks), out_...]
    unnamed x116 -> x120, local copies, waits for them, and re-layouts: 27.5 us -> 24.1 us
  transfers between devices with their start and end apart: 9 -> 3, of which waited for: 8 -> 3; matrix products, arithmetic and copies ran while one was open for 24% -> 7% of each run, Pallas kernels for 0% -> 0%
where the time goes in v1:
time: 678 us; the launch traced here: 666 us
  matrix products  250 us (37%)
  Pallas kernels  137 us (20%)
  waiting for transfers between devices  127 us (19%)
  other arithmetic  85 us (13%)
  local copies, waits for them, and re-layouts  50 us (7%)
  between operations  16.2 us (2%)
    pallas_call x1, Pallas kernels, gather_all(): pl.pallas_call(functools.partial(gather_kernel, nw, zs, ys, chunks), out_...  137 us
    reduce_scatter x1, waiting for transfers between devices, shards(): lax.psum_scatter(accum_up, 'shard', scatter_dimension=0, tiled=True)  71.5 us
    dot_general x9, matrix products, dense_trans(): lax.dot_general(left, right, (((1,), (1,)), ((), ())), preferred_element_...  56.9 us
    dot_general x10, matrix products, dense(): return jnp.dot(left, right, preferred_element_type=jnp.float32)  54.3 us
    convert_element_type x2, other arithmetic, attention_backward(): grad_scores = (probs * (grad_probs - jnp.sum(probs * grad_probs, axis=-1,...  40.2 us
    dot_general x2, matrix products, attention_backward(): jnp.einsum('qhd,khd->hqk', ctx_block, values_all[:stop], preferred_elemen...  37.6 us
    reduce_scatter x1, waiting for transfers between devices, shards(): lax.psum_scatter(accum_down, 'shard', scatter_dimension=0, tiled=True)  32.8 us
    reduce_sum x2, other arithmetic, attention_forward(): total = jnp.sum(expo, axis=-1, keepdims=True)  24.2 us
  transfers between devices with their start and end apart: 3, of which 3 were waited for; matrix products, arithmetic and copies ran while one was open for 7% of the time, Pallas kernels for 0%

profile of v1, /device:TPU:13, one launch (start us, length us, event | category | flops | bytes accessed | tf_op | source)
XLA Modules:
  0.0 665.8 jit_solution(5491241993554674987)
XLA Ops:
  8.0 2.9 copy.42
  12.5 137.3 %gather_weights.1 = (bf16[4,2,128,3072]{3,2,1,0:T(8,128)(2,1)}, bf16[4,2,128,1024]{3,2,1,0:T(8,128)(2,1)}, bf16[4,2,128,4096]{3,2,1,0:T(8,128)(2,1)}, bf16[4,2,5...) custom-call(bf16[128,3072]{1,0:T(8,128)(2,1)} %refs_0_.1, ...), custom_call_target="tpu_custom_call" | custom-call | tf_op jit(solution)/shard_map/gather_weights/pallas_call | solution.py:373
  149.7 1.9 convolution_convert_fusion
  151.7 2.8 fusion.96
  154.5 2.8 fusion.90
  157.3 2.8 fusion.93
  160.1 13.7 %fusion.14 = bf16[1024,3072]{1,0:T(8,128)(2,1)} fusion(f32[1024,1024]{1,0:T(8,128)} %fusion.90, f32[1024,1024]{1,0:T(8,128)} %fusion.93, f32[1024,1024]{1,0:T(8,128)} %fusion.96, bf16[1024,3072]{1,0:T(8,128)(2,1)} %bitcast.205, bf16[1,1024,1024]{1,2,0:T(8,128)(2,1)S(1)} %copy.42, f32[1024]{0:T(1024)S(1)} %copy-done.47, f32[1024]{0:T(1024)S(1)} %fusion.110, ...), kind=kOutput, calls=%fused_computation.29 | convolution fusion | flops 6460276736 | bytes 27275264 | tf_op jit(solution)/shard_map/while/body/eval_jaxpr/dot_general | solution.py:45
  173.8 4.5 fusion.147
  178.4 1.0 copy-done.18
  179.4 2.4 fusion.148
  183.5 4.0 copy.54
  187.4 4.4 copy.52
  191.8 2.3 copy.48
  194.1 2.3 copy.51
  196.4 2.3 copy.47
  198.7 2.3 copy.46
  201.0 3.9 copy.50
  204.9 9.9 %select_reduce_fusion.1 = (f32[16,512]{1,0:T(8,128)S(1)}, f32[16,512,512]{1,2,0:T(8,128)}) fusion(pred[512,512]{0,1:T(8,128)(4,1)S(1)} %iota_compare_fusion.1, bf16[512,16,64]{0,2,1:T(8,128)(2,1)} %bitcast.173, bf16[512,16,64]{0,2,1:T(8,128)(2,1)} %bitcast.169), kind=kOutput, calls=%fused_computation.26 | convolution fusion | flops 549445632 | bytes 19169280 | tf_op jit(solution)/shard_map/while/body/eval_jaxpr/qhd,khd->hqk/dot_general | solution.py:73
  214.8 9.2 %fusion.13 = f32[16,512]{1,0:T(8,128)S(1)} fusion(f32[16,512,512]{1,2,0:T(8,128)} %get-tuple-element.260, f32[16,512]{1,0:T(8,128)S(1)} %get-tuple-element.259, pred[512,512]{0,1:T(8,128)(4,1)S(1)} %iota_compare_fusion.1), kind=kLoop, calls=%fused_computation.27 | loop fusion | flops 16769024 | bytes 17104896 | tf_op jit(solution)/shard_map/while/body/eval_jaxpr/reduce_sum | solution.py:94
  224.6 8.5 %fusion.78 = bf16[16,64,512]{2,1,0:T(8,128)(2,1)S(1)} fusion(bf16[512,16,64]{0,2,1:T(8,128)(2,1)} %bitcast.187, f32[16,512,512]{1,2,0:T(8,128)} %get-tuple-element.260, f32[16,512]{1,0:T(8,128)S(1)} %fusion.13, f32[16,512]{1,0:T(8,128)S(1)} %get-tuple-element.259, pred[512,512]{0,1:T(8,128)(4,1)S(1)} %iota_compare_fusion.1), kind=kOutput, calls=%fused_computation.102 | convolution fusion | flops 558366720 | bytes 19202048 | tf_op jit(solution)/shard_map/while/body/eval_jaxpr/hqk,khd->qhd/dot_general | solution.py:97
  233.1 14.1 %select_reduce_fusion = (f32[16,512]{1,0:T(8,128)S(1)}, f32[16,512,1024]{2,1,0:T(8,128)}) fusion(pred[512,1024]{1,0:T(8,128)(4,1)S(1)} %iota_compare_fusion, bf16[512,16,64]{0,2,1:T(8,128)(2,1)S(1)} %bitcast.164, bf16[1024,16,64]{0,2,1:T(8,128)(2,1)S(1)} %bitcast.157), kind=kOutput, calls=%fused_computation.5 | convolution fusion | flops 1098899456 | bytes 37257216 | tf_op jit(solution)/shard_map/while/body/eval_jaxpr/qhd,khd->hqk/dot_general | solution.py:73
  247.3 15.0 %fusion = f32[16,512]{1,0:T(8,128)S(1)} fusion(f32[16,512,1024]{2,1,0:T(8,128)} %get-tuple-element.258, f32[16,512]{1,0:T(8,128)S(1)} %get-tuple-element.257, pred[512,1024]{1,0:T(8,128)(4,1)S(1)} %iota_compare_fusion), kind=kLoop, calls=%fused_computation.6 | loop fusion | flops 33546240 | bytes 34144256 | tf_op jit(solution)/shard_map/while/body/eval_jaxpr/reduce_sum | solution.py:94
  262.9 14.4 %fusion.79 = bf16[16,64,512]{2,1,0:T(8,128)(2,1)S(1)} fusion(bf16[1024,16,64]{0,2,1:T(8,128)(2,1)S(1)} %bitcast.171, f32[16,512,1024]{2,1,0:T(8,128)} %get-tuple-element.258, f32[16,512]{1,0:T(8,128)S(1)} %fusion, f32[16,512]{1,0:T(8,128)S(1)} %get-tuple-element.257, pred[512,1024]{1,0:T(8,128)(4,1)S(1)} %iota_compare_fusion), kind=kOutput, calls=%fused_computation.103 | convolution fusion | flops 1116209152 | bytes 37289984 | tf_op jit(solution)/shard_map/while/body/eval_jaxpr/hqk,khd->qhd/dot_general | solution.py:97
  277.7 2.2 convolution_convert_fusion.5
  279.9 2.5 fusion.62
  282.4 1.8 fusion.150
  284.9 12.7 %fusion.50 = f32[1024,4096]{1,0:T(8,128)} fusion(bf16[1024,4096]{1,0:T(8,128)(2,1)S(1)} %bitcast.204, f32[1024,1024]{0,1:T(8,128)S(1)} %get-tuple-element.262, f32[1024]{0:T(1024)S(1)} %copy-done.46, f32[1024]{0:T(1024)S(1)} %fusion.111, f32[1024]{0:T(1024)S(1)} %broadcast_multiply_fusion.2), kind=kOutput, calls=%fused_computation.77 | convolution fusion | flops 8594128896 | bytes 29372416 | tf_op jit(solution)/shard_map/while/body/eval_jaxpr/dot_general | solution.py:45
  297.6 29.5 %multiply_reduce_fusion.2 = (f32[1024]{0:T(1024)S(1)}, f32[1024,1024]{0,1:T(8,128)}) fusion(f32[1024,1024]{0,1:T(8,128)} %copy-done.3, f32[1024]{0:T(1024)S(1)} %copy-done.46, f32[1024]{0:T(1024)S(1)} %broadcast_multiply_fusion.2, bf16[1024,4096]{1,0:T(8,128)(2,1)} %bitcast.201, f32[1024,4096]{1,0:T(8,128)} %fusion.50, bf16[4096,1024]{1,0:T(8,128)(2,1)} %bitcast.199, ...), kind=kOutput, calls=%fused_computation.72 | convolution fusion | flops 17271095296 | bytes 44056576 | tf_op jit(solution)/shard_map/while/body/eval_jaxpr/dot_general | solution.py:49
  327.2 4.5 fusion.146
  331.7 0.9 fusion.47
  332.7 1.2 copy-done.2
  333.8 1.6 convolution_convert_fusion.4
  336.1 2.3 fusion.155
  338.5 1.3 fusion.153
  339.8 1.8 add_convert_fusion.1
  341.6 1.5 fusion.149
  343.1 5.6 fusion.75
  348.7 15.3 %fusion.45 = bf16[1024,16,64]{0,2,1:T(8,128)(2,1)S(1)} fusion(f32[512,16,64]{0,2,1:T(8,128)} %fusion.75, bf16[512,16,64]{0,2,1:T(8,128)(2,1)} %bitcast.177, f32[16,512,1024]{2,1,0:T(8,128)} %get-tuple-element.258, f32[16,512]{1,0:T(8,128)S(1)} %copy-done.30, pred[512,1024]{1,0:T(8,128)(4,1)S(1)} %iota_compare_fusion), kind=kOutput, calls=%fused_computation.66 | convolution fusion | flops 1109393408 | bytes 39354368 | tf_op jit(solution)/shard_map/while/body/eval_jaxpr/hqk,qhd->khd/dot_general | solution.py:124
  364.1 1.8 convolution_convert_fusion.1
  365.9 1.3 fusion.100
  367.2 11.9 %multiply_reduce_fusion.1 = (f32[16,512]{1,0:T(8,128)S(1)}, f32[16,512,512]{1,2,0:T(8,128)}) fusion(f32[16,512,512]{1,2,0:T(8,128)} %get-tuple-element.260, f32[16,512]{1,0:T(8,128)S(1)} %copy-done.33, pred[512,512]{0,1:T(8,128)(4,1)S(1)} %copy-done.23, bf16[512,16,64]{0,2,1:T(8,128)(2,1)S(1)} %bitcast.190, bf16[512,16,64]{0,2,1:T(8,128)(2,1)S(1)} %bitcast.188), kind=kOutput, calls=%fused_computation.18 | convolution fusion | flops 557834240 | bytes 35979264 | tf_op jit(solution)/shard_map/while/body/eval_jaxpr/qhd,khd->hqk/dot_general | solution.py:126
  379.2 12.3 %multiply_convert_fusion.1 = bf16[16,512,512]{1,2,0:T(8,128)(2,1)S(1)} fusion(f32[16,512,512]{1,2,0:T(8,128)} %get-tuple-element.266, f32[16,512,512]{1,2,0:T(8,128)} %get-tuple-element.260, f32[16,512]{1,0:T(8,128)S(1)} %get-tuple-element.265, f32[16,512]{1,0:T(8,128)S(1)} %copy-done.33, pred[512,512]{0,1:T(8,128)(4,1)S(1)} %copy-done.23), kind=kLoop, calls=%fused_computation.17 | loop fusion | flops 25165824 | bytes 42270720 | tf_op jit(solution)/shard_map/while/body/eval_jaxpr/convert_element_type | solution.py:131
  391.5 2.4 fusion.80
  393.9 4.0 multiply_bitcast_fusion
  397.9 25.7 %multiply_reduce_fusion = (f32[16,512]{1,0:T(8,128)S(1)}, f32[16,512,1024]{2,1,0:T(8,128)}) fusion(f32[16,512,1024]{2,1,0:T(8,128)} %get-tuple-element.258, f32[16,512]{1,0:T(8,128)S(1)} %copy-done.30, pred[512,1024]{1,0:T(8,128)(4,1)S(1)} %iota_compare_fusion, bf16[512,16,64]{0,2,1:T(8,128)(2,1)S(1)} %bitcast.178, bf16[1024,16,64]{0,2,1:T(8,128)(2,1)S(1)} %bitcast.172), kind=kOutput, calls=%fused_computation.1 | convolution fusion | flops 1115676672 | bytes 70844416 | tf_op jit(solution)/shard_map/while/body/eval_jaxpr/qhd,khd->hqk/dot_general | solution.py:126
  423.6 27.9 %multiply_convert_fusion = bf16[16,512,1024]{2,1,0:T(8,128)(2,1)} fusion(f32[16,512,1024]{2,1,0:T(8,128)} %get-tuple-element.268, f32[16,512,1024]{2,1,0:T(8,128)} %get-tuple-element.258, f32[16,512]{1,0:T(8,128)S(1)} %get-tuple-element.267, f32[16,512]{1,0:T(8,128)S(1)} %copy-done.30, pred[512,1024]{1,0:T(8,128)(4,1)S(1)} %iota_compare_fusion), kind=kLoop, calls=%fused_computation | loop fusion | flops 50331648 | bytes 84475904 | tf_op jit(solution)/shard_map/while/body/eval_jaxpr/convert_element_type | solution.py:131
  451.6 12.0 %fusion.81 = bf16[512,16,64]{0,2,1:T(8,128)(2,1)} fusion(bf16[1024,16,64]{0,2,1:T(8,128)(2,1)S(1)} %bitcast.158, bf16[16,512,1024]{2,1,0:T(8,128)(2,1)} %multiply_convert_fusion), kind=kOutput, calls=%fused_computation.105 | convolution fusion | flops 1074790400 | bytes 19922944 | tf_op jit(solution)/shard_map/while/body/eval_jaxpr/hqk,khd->qhd/dot_general | solution.py:133
  463.6 9.5 %fusion.46 = bf16[1024,16,64]{0,2,1:T(8,128)(2,1)S(1)} fusion(f32[512,16,64]{0,2,1:T(8,128)} %multiply_bitcast_fusion, bf16[512,16,64]{0,2,1:T(8,128)(2,1)S(1)} %bitcast.165, bf16[16,512,1024]{2,1,0:T(8,128)(2,1)} %multiply_convert_fusion), kind=kOutput, calls=%fused_computation.68 | convolution fusion | flops 1076887552 | bytes 22020096 | tf_op jit(solution)/shard_map/while/body/eval_jaxpr/hqk,qhd->khd/dot_general | solution.py:139
  476.9 0.9 copy-done.1
  477.8 0.8 fusion.82
  478.7 2.6 broadcast_multiply_fusion
  482.1 10.9 %fusion.23 = f32[1024,1024]{0,1:T(8,128)S(1)} fusion(bf16[1024,3072]{1,0:T(8,128)(2,1)} %bitcast.206, bf16[1024,1024]{0,1:T(8,128)(2,1)} %bitcast.168, bf16[1024,1024]{0,1:T(8,128)(2,1)} %bitcast.156, bf16[1024,1024]{0,1:T(8,128)(2,1)} %bitcast.161), kind=kOutput, calls=%fused_computation.36 | convolution fusion | flops 6461325312 | bytes 16777216 | tf_op jit(solution)/shard_map/while/body/eval_jaxpr/dot_general | solution.py:49
  493.0 2.1 fusion.41
  495.1 1.9 copy-done.4
  497.0 1.0 fusion.74
  498.0 16.9 %fusion.51 = bf16[1,1024,1024]{1,2,0:T(8,128)(2,1)} fusion(f32[1024,1024]{0,1:T(8,128)} %copy-done.3, f32[1024]{0:T(1024)S(1)} %copy-done.41, bf16[4096,1024]{1,0:T(8,128)(2,1)} %bitcast.200, f32[1024,4096]{1,0:T(8,128)} %fusion.50), kind=kOutput, calls=%fused_computation.78 | convolution fusion | flops 8630829056 | bytes 31461376 | tf_op jit(solution)/shard_map/while/body/eval_jaxpr/dot_general | solution.py:45
  514.9 32.8 %reduce-scatter.3.cloned.1.call-done = f32[128,512]{0,1:T(8,128)} async-done(((f32[1024,512]{0,1:T(8,128)}), f32[128,512]{0,1:T(8,128)}) %reduce-scatter.3.cloned.1.call-update) | async-done | bytes 262160 | tf_op jit(solution)/shard_map/reduce_scatter | solution.py:425
  547.7 71.5 %reduce-scatter.5.cloned.1.call-done = f32[128,512]{0,1:T(8,128)} async-done(((f32[1024,512]{0,1:T(8,128)}), f32[128,512]{0,1:T(8,128)}) %reduce-scatter.5.cloned.1.call-update) | async-done | bytes 262160 | tf_op jit(solution)/shard_map/reduce_scatter | solution.py:426
  619.2 7.2 %fusion.52 = bf16[1,1024,1024]{1,2,0:T(8,128)(2,1)} fusion(f32[1024,1024]{0,1:T(8,128)} %copy-done.2, bf16[1,1024,1024]{1,2,0:T(8,128)(2,1)} %copy.54, f32[1024]{0:T(1024)S(1)} %negate_multiply_fusion, f32[1024]{0:T(1024)S(1)} %copy-done.43, f32[1024]{0:T(1024)S(1)} %copy-done.41, f32[1024]{0:T(1024)S(1)} %multiply_multiply_fusion.2, ...), kind=kLoop, calls=%fused_computation.79 | loop fusion | flops 13631488 | bytes 14704640 | tf_op jit(solution)/shard_map/while/body/jit(dynamic_update_index_in_dim)/broadcast_in_dim | solution.py:410
  626.5 4.1 copy.58
  630.5 2.5 copy.59
  633.1 22.1 %all-reduce.5.cloned.1.call-done = (f32[128,512]{0,1:T(8,128)}, f32[128,512]{0,1:T(8,128)}) async-done(((f32[128,512]{0,1:T(8,128)}, f32[128,512]{0,1:T(8,128)}), (f32[128,512]{0,1:T(8,128)}, f32[128,512]{0,1:T(8,128)})) %all-reduce.5.cloned.1.call-update) | async-done | bytes 524304 | tf_op jit(solution)/shard_map/psum | solution.py:428
  655.2 1.8 copy.60
  657.0 1.8 copy.61
  (144 shorter events, 10.3 us)
Async XLA Ops:
  7.2 540.6 %reduce-scatter.3.cloned.1.call-start = ((), (), s32[]{:S(2)}) async-start(), calls=%async_computation.2 | async-start | bytes 2359296 | tf_op jit(solution)/shard_map/reduce_scatter | solution.py:425
  7.3 217.3 %copy-start.22 = (pred[512,512]{0,1:T(8,128)(4,1)}, pred[512,512]{0,1:T(8,128)(4,1)S(1)}, u32[]{:S(2)}) copy-start(pred[512,512]{0,1:T(8,128)(4,1)S(1)} %iota_compare_fusion.1) | copy-start | bytes 786436
  10.8 271.5 %copy-start = (bf16[1,1024,1024]{1,2,0:T(8,128)(2,1)}, bf16[1,1024,1024]{1,2,0:T(8,128)(2,1)S(1)}, u32[]{:S(2)}) copy-start(bf16[1,1024,1024]{1,2,0:T(8,128)(2,1)S(1)} %copy.42) | copy-start | bytes 6291460
  10.9 138.9 %copy-start.47 = (f32[1024]{0:T(1024)S(1)}, f32[1024]{0:T(1024)}, u32[]{:S(2)}) copy-start(f32[1024]{0:T(1024)} %param.28) | copy-start | bytes 12292
  11.2 148.9 %copy-start.36 = (f32[1024]{0:T(1024)}, f32[1024]{0:T(1024)S(1)}, u32[]{:S(2)}) copy-start(f32[1024]{0:T(1024)S(1)} %broadcast_multiply_fusion.3) | copy-start | bytes 12292
  11.9 0.6 copy-start.38
  12.5 147.7 %copy-start.44 = (f32[1024]{0:T(1024)}, f32[1024]{0:T(1024)S(1)}, u32[]{:S(2)}) copy-start(f32[1024]{0:T(1024)S(1)} %fusion.110) | copy-start | bytes 12292
  149.7 2.0 copy-start.25
  151.7 5.6 copy-start.31
  173.8 5.6 copy-start.18
  224.6 8.5 %copy-start.6 = (bf16[1024,1024]{0,1:T(8,128)(2,1)S(1)}, bf16[1024,1024]{0,1:T(8,128)(2,1)}, u32[]{:S(2)}) copy-start(bf16[1024,1024]{0,1:T(8,128)(2,1)} %copy.52) | copy-start | bytes 6291460
  224.6 8.5 %copy-start.11 = (bf16[512,1024]{0,1:T(8,128)(2,1)S(1)}, bf16[512,1024]{0,1:T(8,128)(2,1)}, u32[]{:S(2)}) copy-start(bf16[512,1024]{0,1:T(8,128)(2,1)} %copy.51) | copy-start | bytes 3145732
  247.3 15.7 %copy-start.16 = (bf16[1024,1024]{0,1:T(8,128)(2,1)S(1)}, bf16[1024,1024]{0,1:T(8,128)(2,1)}, u32[]{:S(2)}) copy-start(bf16[1024,1024]{0,1:T(8,128)(2,1)} %copy.50) | copy-start | bytes 6291460
  277.4 2.5 copy-start.49
  277.6 4.7 copy-start.9
  279.8 4.9 slice-start.4
  279.9 4.9 slice-start.5
  284.2 13.4 %copy-start.3 = (f32[1024,1024]{0,1:T(8,128)}, f32[1024,1024]{0,1:T(8,128)S(1)}, u32[]{:S(2)}) copy-start(f32[1024,1024]{0,1:T(8,128)S(1)} %get-tuple-element.262) | copy-start | bytes 12582916
  284.2 0.7 copy-start.46
  284.9 12.7 %copy-start.13 = (bf16[1,1024,1024]{1,2,0:T(8,128)(2,1)S(1)}, bf16[1,1024,1024]{1,2,0:T(8,128)(2,1)}, u32[]{:S(2)}) copy-start(bf16[1,1024,1024]{1,2,0:T(8,128)(2,1)} %copy.54) | copy-start | bytes 6291460
  284.9 12.7 %copy-start.40 = (f32[1024]{0:T(1024)S(1)}, f32[1024]{0:T(1024)}, u32[]{:S(2)}) copy-start(f32[1024]{0:T(1024)} %fusion.109) | copy-start | bytes 12292
  331.7 2.1 copy-start.2
  331.7 2.1 copy-start.42
  331.7 4.4 copy-start.50
  333.8 9.2 %slice-start = ((s8[16777216]{0:T(1024)(128)(4,1)}), s8[4194304]{0:T(1024)(128)(4,1)S(1)}, s32[]{:S(2)}) async-start(s8[16777216]{0:T(1024)(128)(4,1)} %bitcast.152), calls=%async_computation.5 | async-start | bytes 8388608
  336.1 2.4 copy-start.10
  336.1 7.0 %slice-start.1 = ((s8[16777216]{0:T(1024)(128)(4,1)}), s8[4194304]{0:T(1024)(128)(4,1)S(1)}, s32[]{:S(2)}) async-start(s8[16777216]{0:T(1024)(128)(4,1)} %bitcast.152), calls=%async_computation.6 | async-start | bytes 8388608
  336.1 7.0 %slice-start.2 = ((s8[16777216]{0:T(1024)(128)(4,1)}), s8[4194304]{0:T(1024)(128)(4,1)S(1)}, s32[]{:S(2)}) async-start(s8[16777216]{0:T(1024)(128)(4,1)} %bitcast.152), calls=%async_computation.7 | async-start | bytes 8388608
  339.8 3.3 slice-start.3
  339.8 3.3 copy-start.23
  339.8 3.4 copy-start.33
  343.1 5.6 copy-start.30
  348.7 17.2 %copy-start.32 = (bf16[1024,48]{0,1:T(8,128)(2,1)S(1)}, bf16[1024,48]{0,1:T(8,128)(2,1)}, u32[]{:S(2)}) copy-start(bf16[1024,48]{0,1:T(8,128)(2,1)} %copy-done.31) | copy-start | bytes 294916
  364.1 15.1 %copy-start.14 = (bf16[1024,16,64]{0,2,1:T(8,128)(2,1)}, bf16[1024,16,64]{0,2,1:T(8,128)(2,1)S(1)}, u32[]{:S(2)}) copy-start(bf16[1024,16,64]{0,2,1:T(8,128)(2,1)S(1)} %fusion.45) | copy-start | bytes 6291460
  364.1 3.2 copy-start.27
  364.1 3.1 copy-start.28
  379.2 12.3 %copy-start.15 = (bf16[512,1024]{0,1:T(8,128)(2,1)S(1)}, bf16[512,1024]{0,1:T(8,128)(2,1)}, u32[]{:S(2)}) copy-start(bf16[512,1024]{0,1:T(8,128)(2,1)} %copy.48) | copy-start | bytes 3145732
  391.5 2.5 copy-start.19
  393.9 4.0 copy-start.17
  393.9 4.0 copy-start.24
  423.6 27.9 %copy-start.7 = (bf16[1024,1024]{0,1:T(8,128)(2,1)S(1)}, bf16[1024,1024]{0,1:T(8,128)(2,1)}, u32[]{:S(2)}) copy-start(bf16[1024,1024]{0,1:T(8,128)(2,1)} %copy.52) | copy-start | bytes 6291460
  451.6 12.0 %copy-start.12 = (bf16[512,1024]{0,1:T(8,128)(2,1)S(1)}, bf16[512,1024]{0,1:T(8,128)(2,1)}, u32[]{:S(2)}) copy-start(bf16[512,1024]{0,1:T(8,128)(2,1)} %copy.51) | copy-start | bytes 3145732
  463.6 9.5 %copy-start.26 = (bf16[4,2,128,512]{3,2,1,0:T(8,128)(2,1)S(1)}, bf16[4,2,128,512]{3,2,1,0:T(8,128)(2,1)}, u32[]{:S(2)}) copy-start(bf16[4,2,128,512]{3,2,1,0:T(8,128)(2,1)} %get-tuple-element.231) | copy-start | bytes 3145732
  473.1 2.6 copy-start.5
  473.1 2.0 copy-start.21
  473.1 2.3 copy-start.29
  475.4 2.3 copy-start.1
  475.4 2.3 copy-start.37
  475.4 2.3 copy-start.45
  475.4 2.3 copy-start.48
  475.7 2.9 copy-start.8
  476.2 2.4 copy-start.34
  476.2 2.4 copy-start.35
  481.3 137.9 %reduce-scatter.5.cloned.1.call-start = ((), (), s32[]{:S(2)}) async-start(), calls=%async_computation.3 | async-start | bytes 2359296 | tf_op jit(solution)/shard_map/reduce_scatter | solution.py:426
  482.0 173.2 %all-reduce.5.cloned.1.call-start = ((), (), s32[]{:S(2)}) async-start(), calls=%async_computation.4 | async-start | bytes 1048576 | tf_op jit(solution)/shard_map/psum | solution.py:428
  493.0 2.1 copy-start.39
  495.1 1.9 copy-start.4
  495.1 3.0 copy-start.41
  498.0 121.2 %copy-start.43 = (f32[1024]{0:T(1024)S(1)}, f32[1024]{0:T(1024)}, u32[]{:S(2)}) copy-start(f32[1024]{0:T(1024)} %copy-done.42) | copy-start | bytes 12292
  626.5 4.1 copy-start.20
Sparse Core Ops, SparseCore 0:
  481.4 66.2 reduce-scatter.2
  551.3 67.8 reduce-scatter.4
  621.6 33.5 all-reduce.4

commit v2 on v1

v2 whole, which is shorter than its diff:
```python
import functools

import jax
import jax.numpy as jnp
from jax import lax
from jax.experimental import pallas as pl
from jax.experimental.pallas import tpu as pltpu
from jax.sharding import PartitionSpec as P

MESH = pl.DeviceIdType.MESH

def mesh_split(n_rep, n_shard):
    zs = 4 if n_shard % 4 == 0 else n_shard
    return zs, n_shard // zs

def share_rows(rows):
    return max(16, rows * 3 // 8 // 16 * 16)

def chunk_list(shapes, width):
    out = []
    for w, (rows, cols) in enumerate(shapes):
        for r0 in range(0, rows, 128):
            for c0 in range(0, cols, width):
                out.append((w, r0, min(rows, 128), c0, min(width, cols)))
    return out

def gather_kernel(n_w, zs, ys, chunks, *refs):
    ins = refs[:n_w]
    outs = refs[n_w:2 * n_w]
    zsend, zrecv, ysend, yrecv, xsend, xrecv, csend, crecv, lsem = refs[2 * n_w:]
    r = lax.axis_index("rep")
    s = lax.axis_index("shard")
    z, y = s // ys, lax.rem(s, ys)
    core = lax.rem(r, 2)
    xp = lax.rem(r // 2, 2)
    sib = r + 1 - 2 * core
    par = r + 2 - 4 * xp
    zpeers = [lax.rem(z + k, zs) for k in range(1, zs)]
    ypeers = [lax.rem(y + k, ys) for k in range(1, ys)]
    peers = [(r, zz * ys + y) for zz in zpeers] + [(r, z * ys + yy) for yy in ypeers] + [(par, s), (sib, s)]
    local = []
    for w in range(n_w):
        cp = pltpu.make_async_copy(ins[w], outs[w].at[z, y], lsem.at[w])
        cp.start()
        local.append(cp)
    bar = pltpu.get_barrier_semaphore()
    for p in peers:
        pl.semaphore_signal(bar, inc=1, device_id=p, device_id_type=MESH)
    pl.semaphore_wait(bar, len(peers))

    def rdma(src, dst, ss, rs, dev):
        cp = pltpu.make_async_remote_copy(src_ref=src, dst_ref=dst, send_sem=ss, recv_sem=rs, device_id=dev, device_id_type=MESH)
        cp.start()

    def geom(t):
        w, r0, rows, c0, cols = chunks[t]
        a = share_rows(rows)
        half = cols // 2
        mine = pl.ds(pl.multiple_of(r0 + xp * a, 16), rows - a)
        excl = pl.ds(pl.multiple_of(r0 + xp * (rows - a), 16), a)
        missing = pl.ds(pl.multiple_of(r0 + (1 - xp) * (rows - a), 16), a)
        col = pl.ds(pl.multiple_of(c0 + core * half, 128), half)
        return w, a, half, rows, mine, excl, missing, col

    def wait_total(elems, sem):
        for out in outs:
            _, _, big_r, big_n = out.shape
            for lead in range(1, zs + 1):
                for take in range(big_r, 0, -16):
                    if elems % (lead * take * 128) == 0 and elems // (lead * take) <= big_n:
                        reg = out.at[pl.ds(0, lead), 0, pl.ds(0, take), pl.ds(0, elems // (lead * take))]
                        pltpu.make_async_copy(reg, reg, sem).wait()
                        return
        raise ValueError("no region")

    def stage_z(t):
        w, a, half, rows, mine, excl, missing, col = geom(t)
        for zz in zpeers:
            rdma(ins[w].at[mine, col], outs[w].at[z, y, mine, col], zsend.at[t], zrecv.at[t], (r, zz * ys + y))

    def stage_y(t):
        w, a, half, rows, mine, excl, missing, col = geom(t)
        wait_total((zs - 1) * (rows - a) * half, zrecv.at[t])
        for yy in ypeers:
            rdma(outs[w].at[:, y, mine, col], outs[w].at[:, y, mine, col], ysend.at[t], yrecv.at[t], (r, z * ys + yy))
        for zz in zpeers:
            rdma(outs[w].at[zz, y, excl, col], outs[w].at[zz, y, excl, col], xsend.at[t], xrecv.at[t], (par, s))
            rdma(outs[w].at[zz, y, mine, col], outs[w].at[zz, y, mine, col], csend.at[t], crecv.at[t], (sib, s))

    def stage_x(t):
        w, a, half, rows, mine, excl, missing, col = geom(t)
        wait_total((ys - 1) * zs * (rows - a) * half, yrecv.at[t])
        for yy in ypeers:
            rdma(outs[w].at[:, yy, excl, col], outs[w].at[:, yy, excl, col], xsend.at[t], xrecv.at[t], (par, s))
            rdma(outs[w].at[:, yy, mine, col], outs[w].at[:, yy, mine, col], csend.at[t], crecv.at[t], (sib, s))

    def stage_c(t):
        w, a, half, rows, mine, excl, missing, col = geom(t)
        wait_total((zs * ys - 1) * a * half, xrecv.at[t])
        for zz in zpeers:
            rdma(outs[w].at[zz, y, missing, col], outs[w].at[zz, y, missing, col], csend.at[t], crecv.at[t], (sib, s))
        for yy in ypeers:
            rdma(outs[w].at[:, yy, missing, col], outs[w].at[:, yy, missing, col], csend.at[t], crecv.at[t], (sib, s))

    n = len(chunks)
    for t in range(n):
        stage_z(t)
    for cp in local:
        cp.wait()
    for t in range(n + 2):
        if t < n:
            stage_y(t)
        if 0 <= t - 1 < n:
            stage_x(t - 1)
        if 0 <= t - 2 < n:
            stage_c(t - 2)
    for t in range(n):
        w, a, half, rows, mine, excl, missing, col = geom(t)
        wait_total((zs * ys - 1) * rows * half, crecv.at[t])
        wait_total((zs * ys - 1) * rows * half, csend.at[t])
        wait_total((zs * ys - 1) * a * half, xsend.at[t])
        wait_total((zs - 1) * (rows - a) * half, zsend.at[t])
        wait_total((ys - 1) * zs * (rows - a) * half, ysend.at[t])


def gather_all(shards, n_rep, n_shard, width=1024, cid=0):
    zs, ys = mesh_split(n_rep, n_shard)
    chunks = chunk_list([w.shape for w in shards], width)
    n = len(chunks)
    nw = len(shards)
    res = pl.pallas_call(
        functools.partial(gather_kernel, nw, zs, ys, chunks),
        out_shape=[jax.ShapeDtypeStruct((zs, ys) + w.shape, w.dtype) for w in shards],
        in_specs=[pl.BlockSpec(memory_space=pltpu.VMEM)] * nw,
        out_specs=[pl.BlockSpec(memory_space=pl.ANY)] * nw,
        scratch_shapes=[pltpu.SemaphoreType.DMA((n,))] * 8 + [pltpu.SemaphoreType.DMA((nw,))],
        compiler_params=pltpu.CompilerParams(collective_id=cid, has_side_effects=True),
        name="gather_weights",
    )(*shards)
    return [v.reshape((-1, v.shape[-1])) for v in res]


EPS = 1e-05
HEAD = 64
RANK = 16
ADAPTERS = 8
COLS = 4 * RANK
VMEM_CAP = 60 * 1024 * 1024
BF = jnp.bfloat16
F32 = jnp.float32


def dense(left, right):
    return jnp.dot(left, right, preferred_element_type=F32)


def dense_trans(left, right):
    return lax.dot_general(left, right, (((1,), (1,)), ((), ())), preferred_element_type=F32)


def dense_left(left, right):
    return lax.dot_general(left, right, (((0,), (0,)), ((), ())), preferred_element_type=F32)


def lane_group(values, size, group):
    lanes = lax.broadcasted_iota(jnp.int32, values.shape, 1)
    return jnp.where(lanes // size == group, values, jnp.zeros_like(values))


def norm_stats(values):
    center = values - jnp.mean(values, axis=-1, keepdims=True)
    rs = lax.rsqrt(jnp.mean(center * center, axis=-1, keepdims=True) + EPS)
    return center * rs, rs


def norm_back(unit, rs, gain, grad):
    eg = grad * gain
    return rs * (eg - jnp.mean(eg, axis=-1, keepdims=True) - unit * jnp.mean(eg * unit, axis=-1, keepdims=True))


def qkv_body(per_third, x_ref, g_ref, w_ref, down_ref, up_ref, normed_ref, inner_ref, out_ref):
    step = pl.program_id(0)
    rows = 256

    @pl.when(step == 0)
    def _():
        for i in range(x_ref.shape[0] // rows):
            sl = pl.ds(i * rows, rows)
            unit, _ = norm_stats(x_ref[sl, :].astype(F32))
            normed_ref[sl, :] = (unit * g_ref[...]).astype(BF)
            inner_ref[sl, :] = dense(normed_ref[sl, :], down_ref[...]).astype(BF)

    inner = lane_group(inner_ref[...], RANK, step // per_third)
    out_ref[...] = (dense(normed_ref[...], w_ref[...]) + dense_trans(inner, up_ref[...])).astype(BF)


def qkv_forward(x, gain, qkv, down, up):
    seq, dim = x.shape
    total = qkv.shape[1]
    block = min(512, dim)
    per_third = dim // block
    return pl.pallas_call(
        functools.partial(qkv_body, per_third),
        grid=(total // block,),
        out_shape=[
            jax.ShapeDtypeStruct((seq, dim), BF),
            jax.ShapeDtypeStruct((seq, COLS), BF),
            jax.ShapeDtypeStruct((seq, total), BF),
        ],
        in_specs=[
            pl.BlockSpec((seq, dim), lambda j: (0, 0), pipeline_mode=pl.Buffered(1)),
            pl.BlockSpec((1, dim), lambda j: (0, 0)),
            pl.BlockSpec((dim, block), lambda j: (0, j)),
            pl.BlockSpec((dim, COLS), lambda j: (0, 0)),
            pl.BlockSpec((block, COLS), lambda j: (lax.rem(j, per_third), 0)),
        ],
        out_specs=[
            pl.BlockSpec((seq, dim), lambda j: (0, 0)),
            pl.BlockSpec((seq, COLS), lambda j: (0, 0)),
            pl.BlockSpec((seq, block), lambda j: (0, j)),
        ],
        compiler_params=pltpu.CompilerParams(vmem_limit_bytes=VMEM_CAP),
        name="qkv_forward",
    )(x, gain, qkv, down, up)


def attn_fwd_body(tile, q_ref, k_ref, v_ref, ctx_ref, p_ref):
    seq, lanes = q_ref.shape
    heads = lanes // HEAD
    scale = HEAD ** (-0.5)
    rows = lax.broadcasted_iota(jnp.int32, (tile, tile), 0)
    cols = lax.broadcasted_iota(jnp.int32, (tile, tile), 1)
    keep = rows >= cols
    off = 0
    for i in range(seq // tile):
        stop = (i + 1) * tile
        q = q_ref[pl.ds(i * tile, tile), :] * jnp.asarray(scale, BF)
        acc = None
        for h in range(heads):
            qh = lane_group(q, HEAD, h)
            s = dense_trans(qh, k_ref[pl.ds(0, stop), :])
            diag = jnp.where(keep, s[:, stop - tile :], -1e30)
            s = diag if i == 0 else jnp.concatenate([s[:, : stop - tile], diag], axis=1)
            peak = jnp.max(s, axis=-1, keepdims=True)
            e = jnp.exp(s - peak)
            inv = 1.0 / jnp.sum(e, axis=-1, keepdims=True)
            p = (e * inv).astype(BF)
            p_ref[h, :, pl.ds(off, stop)] = p
            o = dense(p, lane_group(v_ref[pl.ds(0, stop), :], HEAD, h))
            acc = o if acc is None else acc + o
        ctx_ref[pl.ds(i * tile, tile), :] = acc.astype(BF)
        off += stop


def attention_forward(proj, tile, lanes=128):
    seq = proj.shape[0]
    width = proj.shape[1] // 3
    n = width // lanes
    heads = lanes // HEAD
    packed = tile * (seq // tile) * (seq // tile + 1) // 2
    return pl.pallas_call(
        functools.partial(attn_fwd_body, tile),
        grid=(n,),
        out_shape=[
            jax.ShapeDtypeStruct((seq, width), BF),
            jax.ShapeDtypeStruct((width // HEAD, tile, packed), BF),
        ],
        in_specs=[pl.BlockSpec((seq, lanes), lambda j, t=t: (0, t * n + j)) for t in range(3)],
        out_specs=[
            pl.BlockSpec((seq, lanes), lambda j: (0, j)),
            pl.BlockSpec((heads, tile, packed), lambda j: (j, 0, 0)),
        ],
        compiler_params=pltpu.CompilerParams(vmem_limit_bytes=VMEM_CAP),
        name="attention_forward",
    )(proj, proj, proj)


def attn_bwd_body(tile, q_ref, k_ref, v_ref, go_ref, ctx_ref, p_ref, dq_ref, dk_ref, dv_ref, dk_acc, dv_acc):
    seq, lanes = q_ref.shape
    heads = lanes // HEAD
    scale = HEAD ** (-0.5)
    off = 0
    n = seq // tile
    dk_acc[...] = jnp.zeros_like(dk_acc)
    dv_acc[...] = jnp.zeros_like(dv_acc)
    for i in range(n):
        stop = (i + 1) * tile
        sl = pl.ds(i * tile, tile)
        past = pl.ds(0, stop)
        go = go_ref[sl, :]
        q = q_ref[sl, :]
        prod = go.astype(F32) * ctx_ref[sl, :].astype(F32)
        acc = None
        for h in range(heads):
            delta = jnp.sum(lane_group(prod, HEAD, h), axis=-1, keepdims=True)
            gh = lane_group(go, HEAD, h)
            p = p_ref[h, :, pl.ds(off, stop)]
            dp = dense_trans(gh, v_ref[past, :])
            ds = (p.astype(F32) * (dp - delta)).astype(BF)
            dv_acc[past, :] += dense_left(p, gh)
            dk_acc[past, :] += dense_left(ds, lane_group(q, HEAD, h))
            o = dense(ds, lane_group(k_ref[past, :], HEAD, h))
            acc = o if acc is None else acc + o
        dq_ref[sl, :] = (acc * scale).astype(BF)
        off += stop
    dk_ref[...] = (dk_acc[...] * scale).astype(BF)
    dv_ref[...] = dv_acc[...].astype(BF)


def attention_backward(proj, grad_ctx, ctx, probs, tile, lanes=128):
    seq = proj.shape[0]
    width = proj.shape[1] // 3
    n = width // lanes
    heads = lanes // HEAD
    packed = probs.shape[2]
    blk = pl.BlockSpec((seq, lanes), lambda j: (0, j))
    return pl.pallas_call(
        functools.partial(attn_bwd_body, tile),
        grid=(n,),
        out_shape=[jax.ShapeDtypeStruct((seq, width), BF)] * 3,
        in_specs=[pl.BlockSpec((seq, lanes), lambda j, t=t: (0, t * n + j)) for t in range(3)]
        + [blk, blk, pl.BlockSpec((heads, tile, packed), lambda j: (j, 0, 0))],
        out_specs=[blk] * 3,
        scratch_shapes=[pltpu.VMEM((seq, lanes), F32)] * 2,
        compiler_params=pltpu.CompilerParams(vmem_limit_bytes=VMEM_CAP),
        name="attention_backward",
    )(proj, proj, proj, grad_ctx, ctx, probs)


def mlp_body(
    chunk, len_ref, x_ref, ctx_ref, cot_ref, g_ref, out_w, up_w, down_w, adn_ref, aup_ref,
    y_ref, gh_ref, gc_ref, dgrad_ref, ugrad_ref, nt_ref, mlp_acc, gn_acc,
):
    step = pl.program_id(0)
    rows = x_ref.shape[0]
    ctx = ctx_ref[...]
    inner_out = lane_group(dense(ctx, adn_ref[...]), RANK, 3).astype(BF)
    hidden = x_ref[...].astype(F32) + (dense(ctx, out_w[...]) + dense_trans(inner_out, aup_ref[...]))
    unit, rs = norm_stats(hidden)
    nt_ref[...] = (unit * g_ref[...]).astype(BF)
    pos = step * rows + lax.broadcasted_iota(jnp.int32, (rows, 1), 0)
    valid = pos < len_ref[0]
    cot = cot_ref[...]
    grad_mlp = jnp.where(valid, cot, jnp.zeros_like(cot))
    ff = up_w.shape[1]
    mlp_acc[...] = jnp.zeros_like(mlp_acc)
    gn_acc[...] = jnp.zeros_like(gn_acc)

    def one(f, carry):
        fs = pl.ds(pl.multiple_of(f * chunk, chunk), chunk)
        u = dense(nt_ref[...], up_w[:, fs])
        ga = dense_trans(grad_mlp, down_w[fs, :])
        k = 0.7978845608028654
        sq = u * u
        t = jnp.tanh(k * (u + 0.044715 * u * sq))
        half = 0.5 * (1.0 + t)
        act = (u * half).astype(BF)
        d = half + 0.5 * u * (1.0 - t * t) * (k * (1.0 + (3.0 * 0.044715) * sq))
        gp = (ga * d).astype(BF)
        mlp_acc[...] += dense(act, down_w[fs, :])
        gn_acc[...] += dense_trans(gp, up_w[:, fs])
        return carry

    lax.fori_loop(0, ff // chunk, one, 0, unroll=2)
    y_ref[...] = jnp.where(valid, hidden + mlp_acc[...], 0.0).astype(BF)
    gh = grad_mlp.astype(F32) + norm_back(unit, rs, g_ref[...], gn_acc[...])
    gh_ref[...] = gh
    ga = gh.astype(BF)
    gio = lane_group(dense(ga, aup_ref[...]), RANK, 3).astype(BF)
    gc_ref[...] = (dense_trans(ga, out_w[...]) + dense_trans(gio, adn_ref[...])).astype(BF)

    @pl.when(step == 0)
    def _():
        dgrad_ref[...] = jnp.zeros_like(dgrad_ref)
        ugrad_ref[...] = jnp.zeros_like(ugrad_ref)

    dgrad_ref[...] += dense_left(gio, ctx)
    ugrad_ref[...] += dense_left(inner_out, ga)


def mlp_both(length, x, ctx, cot, gain, out_w, up_w, down_w, adn, aup, rows=256, chunk=512):
    seq, dim = x.shape
    ff = up_w.shape[1]
    row = pl.BlockSpec((rows, dim), lambda i: (i, 0))

    def whole(shape):
        return pl.BlockSpec(shape, lambda i: (0, 0), pipeline_mode=pl.Buffered(1))

    return pl.pallas_call(
        functools.partial(mlp_body, chunk),
        grid=(seq // rows,),
        out_shape=[
            jax.ShapeDtypeStruct((seq, dim), BF),
            jax.ShapeDtypeStruct((seq, dim), F32),
            jax.ShapeDtypeStruct((seq, dim), BF),
            jax.ShapeDtypeStruct((COLS, dim), F32),
            jax.ShapeDtypeStruct((COLS, dim), F32),
        ],
        in_specs=[
            pl.BlockSpec(memory_space=pltpu.SMEM),
            row, row, row,
            whole((1, dim)), whole((dim, dim)), whole((dim, ff)), whole((ff, dim)), whole((dim, COLS)), whole((dim, COLS)),
        ],
        out_specs=[row, row, row, whole((COLS, dim)), whole((COLS, dim))],
        scratch_shapes=[pltpu.VMEM((rows, dim), BF), pltpu.VMEM((rows, dim), F32), pltpu.VMEM((rows, dim), F32)],
        compiler_params=pltpu.CompilerParams(vmem_limit_bytes=VMEM_CAP),
        name="mlp_forward_backward",
    )(length, x, ctx, cot, gain, out_w, up_w, down_w, adn, aup)


def tail_body(
    x_ref, gh_ref, normed_ref, inner_ref, dq_ref, dk_ref, dv_ref, g_ref, w_ref, adn_ref, aup_ref, din_ref, uin_ref,
    id_ref, gx_ref, pay_ref, dgrad_ref, ugrad_ref,
):
    step = pl.program_id(0)
    dim = x_ref.shape[1]
    thirds = [dq_ref[...], dk_ref[...], dv_ref[...]]
    gi = None
    gn = None
    for p in range(3):
        one = lane_group(dense(thirds[p], aup_ref[...]), RANK, p)
        gi = one if gi is None else gi + one
        g = dense_trans(thirds[p], w_ref[:, pl.ds(p * dim, dim)])
        gn = g if gn is None else gn + g
    gi = gi.astype(BF)
    gn = gn + dense_trans(gi, adn_ref[...])
    unit, rs = norm_stats(x_ref[...].astype(F32))
    gx_ref[...] = (gh_ref[...] + norm_back(unit, rs, g_ref[...], gn)).astype(BF)

    @pl.when(step == 0)
    def _():
        dgrad_ref[...] = din_ref[...]
        ugrad_ref[...] = uin_ref[...]

    dgrad_ref[...] += dense_left(gi, normed_ref[...])
    up = None
    for p in range(3):
        one = dense_left(lane_group(inner_ref[...], RANK, p), thirds[p])
        up = one if up is None else up + one
    ugrad_ref[...] += up

    @pl.when(step == pl.num_programs(0) - 1)
    def _():
        n, pay, width = pay_ref.shape
        mark = jnp.full((pay - 2 * COLS, width), id_ref[0], jnp.int32).astype(F32)
        for i in range(n):
            sl = pl.ds(i * width, width)
            pay_ref[i] = jnp.concatenate([dgrad_ref[:, sl], ugrad_ref[:, sl], mark], axis=0).astype(BF)


def tail_backward(x, gh, normed, inner, dq, dk, dv, gain, qkv, adn, aup, din, uin, adapter, n_shard, rows=256):
    seq, dim = x.shape
    row = pl.BlockSpec((rows, dim), lambda i: (i, 0))

    def whole(shape):
        return pl.BlockSpec(shape, lambda i: (0, 0), pipeline_mode=pl.Buffered(1))

    return pl.pallas_call(
        tail_body,
        grid=(seq // rows,),
        out_shape=[
            jax.ShapeDtypeStruct((seq, dim), BF),
            jax.ShapeDtypeStruct((n_shard, PAY, dim // n_shard), BF),
        ],
        in_specs=[
            row, row, row, pl.BlockSpec((rows, COLS), lambda i: (i, 0)), row, row, row,
            whole((1, dim)), whole(qkv.shape), whole((dim, COLS)), whole((dim, COLS)), whole((COLS, dim)), whole((COLS, dim)),
            pl.BlockSpec(memory_space=pltpu.SMEM),
        ],
        out_specs=[row, pl.BlockSpec((n_shard, PAY, dim // n_shard), lambda i: (0, 0, 0))],
        scratch_shapes=[pltpu.VMEM((COLS, dim), F32)] * 2,
        compiler_params=pltpu.CompilerParams(vmem_limit_bytes=VMEM_CAP),
        name="tail_backward",
    )(x, gh, normed, inner, dq, dk, dv, gain, qkv, adn, aup, din, uin, adapter)


def one_slot(tokens, slot_cot, length, adapter, weights, gain_one, gain_two, n_shard):
    qkv, out_w, up_w, down_w, adapter_down, adapter_up = weights
    first = adapter * COLS
    adn = lax.dynamic_slice_in_dim(adapter_down, first, COLS, 1)
    aup = lax.dynamic_slice_in_dim(adapter_up, first, COLS, 1)
    tile = 256 if tokens.shape[0] % 256 == 0 else tokens.shape[0]
    g_one, g_two = gain_one[None], gain_two[None]
    normed, inner, proj = qkv_forward(tokens, g_one, qkv, adn, aup)
    ctx, probs = attention_forward(proj, tile)
    y, gh, gc, dg, ug = mlp_both(length, tokens, ctx, slot_cot, g_two, out_w, up_w, down_w, adn, aup)
    dq, dk, dv = attention_backward(proj, gc, ctx, probs, tile)
    gx, pay = tail_backward(
        tokens, gh, normed, inner, dq, dk, dv, g_one, qkv, adn, aup, dg, ug, adapter[None], n_shard
    )
    return y, gx, pay


PAY = 2 * COLS + 16


def flip(value, bit):
    return value + bit - 2 * bit * lax.rem(value // bit, 2)


def reduce_body(n_rep, n_shard, bits, pay_ref, down_ref, up_ref, buf, send, recv, xsend, xrecv, lsem):
    r = lax.axis_index("rep")
    s = lax.axis_index("shard")
    others = [lax.rem(s + k, n_shard) for k in range(1, n_shard)]
    peers = [(r, o) for o in others] + [(flip(r, b), s) for b in bits]
    own = pltpu.make_async_copy(pay_ref.at[s], buf.at[r, s], lsem)
    own.start()
    bar = pltpu.get_barrier_semaphore()
    for p in peers:
        pl.semaphore_signal(bar, inc=1, device_id=p, device_id_type=MESH)
    pl.semaphore_wait(bar, len(peers))
    copies = []
    for k, o in enumerate(others):
        cp = pltpu.make_async_remote_copy(
            src_ref=pay_ref.at[o], dst_ref=buf.at[r, s], send_sem=send.at[k], recv_sem=recv.at[k],
            device_id=(r, o), device_id_type=MESH,
        )
        cp.start()
        copies.append(cp)
    own.wait()
    for cp in copies:
        cp.wait()
    held = [0]
    at = 0
    for b in bits:
        partner = flip(r, b)
        copies = []
        for m in held:
            q = r
            for c in bits:
                if m & c:
                    q = flip(q, c)
            cp = pltpu.make_async_remote_copy(
                src_ref=buf.at[q], dst_ref=buf.at[q], send_sem=xsend.at[at], recv_sem=xrecv.at[at],
                device_id=(partner, s), device_id_type=MESH,
            )
            cp.start()
            copies.append(cp)
            at += 1
        for cp in copies:
            cp.wait()
        held = held + [m | b for m in held]
    rows = buf.shape[3]
    for a in range(ADAPTERS):

        def add(i, acc):
            low = buf[i // n_shard, lax.rem(i, n_shard)]
            block = low[: 2 * COLS, :].astype(F32)
            mark = low[2 * COLS : 2 * COLS + 8, :].astype(F32)[0:1, :]
            return acc + jnp.where(mark == float(a), block, 0.0)

        total = lax.fori_loop(0, n_rep * n_shard, add, jnp.zeros((2 * COLS, rows), F32), unroll=4)
        flat = jnp.transpose(total)
        down_ref[:, pl.ds(a * COLS, COLS)] = flat[:, :COLS]
        up_ref[:, pl.ds(a * COLS, COLS)] = flat[:, COLS:]


def reduce_grads(pay, n_rep, n_shard):
    bits = [1 << k for k in range(1, n_rep.bit_length() - 1)] + [1]
    rows = pay.shape[2]
    return pl.pallas_call(
        functools.partial(reduce_body, n_rep, n_shard, bits),
        out_shape=[jax.ShapeDtypeStruct((rows, ADAPTERS * COLS), F32)] * 2,
        in_specs=[pl.BlockSpec(memory_space=pltpu.VMEM)],
        out_specs=[pl.BlockSpec(memory_space=pltpu.VMEM)] * 2,
        scratch_shapes=[pltpu.VMEM((n_rep, n_shard, PAY, rows), BF)]
        + [pltpu.SemaphoreType.DMA((n_shard - 1,))] * 2
        + [pltpu.SemaphoreType.DMA((n_rep - 1,))] * 2
        + [pltpu.SemaphoreType.DMA],
        compiler_params=pltpu.CompilerParams(collective_id=1, has_side_effects=True, vmem_limit_bytes=VMEM_CAP),
        name="reduce_grads",
    )(pay)


def shards(
    inputs,
    cotangent,
    lengths,
    adapter_ids,
    gain_one,
    gain_two,
    qkv_weight,
    out_weight,
    up_weight,
    down_weight,
    adapter_down,
    adapter_up,
):
    n_rep, n_shard = lax.axis_size("rep"), lax.axis_size("shard")
    weights = gather_all(
        (qkv_weight, out_weight, up_weight, down_weight, adapter_down, adapter_up), n_rep, n_shard
    )
    output, grad, pay = one_slot(
        inputs[0], cotangent[0], lengths, adapter_ids[0], weights, gain_one, gain_two, n_shard
    )
    down_grad, up_grad = reduce_grads(pay, n_rep, n_shard)
    return (output[None], grad[None], down_grad, up_grad)


def solution(mesh):
    return jax.shard_map(
        shards,
        mesh=mesh,
        in_specs=(
            P(("rep", "shard"), None, None),
            P(("rep", "shard"), None, None),
            P(("rep", "shard")),
            P(("rep", "shard")),
            P(),
            P(),
            P("shard", None),
            P("shard", None),
            P("shard", None),
            P("shard", None),
            P("shard", None),
            P("shard", None),
        ),
        out_specs=(
            P(("rep", "shard"), None, None),
            P(("rep", "shard"), None, None),
            P("shard", None),
            P("shard", None),
        ),
        check_vma=False,
    )
```

time: 678 us -> 327 us (0.48); the launches traced: 666 us -> 327 us
  matrix products: 250 us -> 0 us
  Pallas kernels: 137 us -> 319 us
  waiting for transfers between devices: 127 us -> 0 us
  other arithmetic: 85 us -> 0 us
  local copies, waits for them, and re-layouts: 50 us -> 5.38 us
  between operations: 16.2 us -> 1.96 us
    dot_general x37 -> x0, matrix products: 250 us -> none  [the longest x9 56.9 us: dense_trans(): lax.dot_general(left, right, (((1,), (1,)), ((), ())), preferred_element_...]
    pallas_call x0 -> x6, Pallas kernels: none -> 182 us  [the longest x1 63.3 us: mlp_both(): pl.pallas_call(functools.partial(mlp_body, chunk), grid=(seq // rows,), o...]
    reduce_scatter x2 -> x0, waiting for transfers between devices: 104 us -> none  [the longest x1 71.5 us: shards(): lax.psum_scatter(accum_up, 'shard', scatter_dimension=0, tiled=True)]
    convert_element_type x4 -> x0, other arithmetic: 41.7 us -> none  [the longest x2 40.2 us: attention_backward(): grad_scores = (probs * (grad_probs - jnp.sum(probs * grad_probs, axis=-1,...]
    reduce_sum x7 -> x0, other arithmetic: 31.2 us -> none  [the longest x2 24.2 us: attention_forward(): total = jnp.sum(expo, axis=-1, keepdims=True)]
    slice x9 -> x0, local copies, waits for them, and re-layouts: 25.9 us -> none  [the longest x2 6.86 us: split_heads(): keys_all = projected[:, width:2 * width].reshape(seq, HEADS, head_size)]
    psum x1 -> x0, waiting for transfers between devices: 22.1 us -> none  [shards(): summed = lax.psum((owned[0], owned[1]), 'rep')]
    unnamed x120 -> x2, local copies, waits for them, and re-layouts: 24.1 us -> 3.34 us
  transfers between devices with their start and end apart: 3 -> 0, of which waited for: 3 -> 0; matrix products, arithmetic and copies ran while one was open for 7% -> 0% of each run, Pallas kernels for 0% -> 0%
where the time goes in v2:
time: 327 us
  Pallas kernels  319 us (98%)
  local copies, waits for them, and re-layouts  5.38 us (2%)
    pallas_call x1, Pallas kernels, gather_all(): pl.pallas_call(functools.partial(gather_kernel, nw, zs, ys, chunks), out_...  137 us
    pallas_call x1, Pallas kernels, mlp_both(): pl.pallas_call(functools.partial(mlp_body, chunk), grid=(seq // rows,), o...  63.3 us
    pallas_call x1, Pallas kernels, attention_backward(): pl.pallas_call(functools.partial(attn_bwd_body, tile), grid=(n,), out_sha...  32.6 us
    pallas_call x1, Pallas kernels, attention_forward(): pl.pallas_call(functools.partial(attn_fwd_body, tile), grid=(n,), out_sha...  27.5 us
    pallas_call x1, Pallas kernels, reduce_grads(): pl.pallas_call(functools.partial(reduce_body, n_rep, n_shard, bits), out_...  25.9 us
    pallas_call x1, Pallas kernels, tail_backward(): pl.pallas_call(tail_body, grid=(seq // rows,), out_shape=[jax.ShapeDtypeS...  18.2 us
    pallas_call x1, Pallas kernels, qkv_forward(): pl.pallas_call(functools.partial(qkv_body, per_third), grid=(total // blo...  14.6 us

profile of v2, /device:TPU:13, one launch (start us, length us, event | category | flops | bytes accessed | tf_op | source)
XLA Modules:
  0.0 326.7 jit_solution(9156603149159237085)
XLA Ops:
  1.9 137.3 %gather_weights.1 = (bf16[4,2,128,3072]{3,2,1,0:T(8,128)(2,1)}, bf16[4,2,128,1024]{3,2,1,0:T(8,128)(2,1)}, bf16[4,2,128,4096]{3,2,1,0:T(8,128)(2,1)}, bf16[4,2,5...) custom-call(bf16[128,3072]{1,0:T(8,128)(2,1)} %refs_0_.1, ...), custom_call_target="tpu_custom_call" | custom-call | tf_op jit(solution)/shard_map/gather_weights/pallas_call | solution.py:131
  139.2 2.0 constant_dynamic-slice_fusion
  141.2 14.6 %qkv_forward.1 = (bf16[1024,1024]{1,0:T(8,128)(2,1)}, bf16[1024,64]{1,0:T(8,128)(2,1)}, bf16[1024,3072]{1,0:T(8,128)(2,1)}) custom-call(bf16[1024,1024]{1,0:T(8,128)(2,1)} %bitcast.15, f32[1,1024]{1,0:T(1,128)} %bitcast.24, bf16[1024,3072]{1,0:T(8,128)(2,1)} %bitcast.13, bf16[1024,64]{1,0:T(8,128)(2,1)} %get-tuple-element.51.down_ref.adn_ref, ...), custom_call_target="tpu_custom_call" | custom-call | tf_op jit(solution)/shard_map/qkv_forward/pallas_call | solution.py:202
  155.8 27.5 %attention_forward.1 = (bf16[1024,1024]{1,0:T(8,128)(2,1)}, bf16[16,256,2560]{2,1,0:T(8,128)(2,1)}) custom-call(bf16[1024,3072]{1,0:T(8,128)(2,1)} %get-tuple-element.30.q_ref.k_ref.v_ref, bf16[1024,3072]{1,0:T(8,128)(2,1)} %get-tuple-element.30.q_ref.k_ref.v_ref, bf16[1024,3072]{1,0:T(8,128)(2,1)} %get-tuple-element.30.q_ref.k_ref.v_ref), custom_call_target="tpu_custom_call" | custom-call | tf_op jit(solution)/shard_map/attention_forward/pallas_call | solution.py:261
  183.4 63.3 %mlp_forward_backward.1 = (bf16[1024,1024]{1,0:T(8,128)(2,1)}, f32[1024,1024]{1,0:T(8,128)}, bf16[1024,1024]{1,0:T(8,128)(2,1)}, f32[64,1024]{1,0:T(8,128)}, f32[64,1024]{1,0:T(8,128)}) custom-call(s32[1]{0:T(128)S(6)} %copy.18.len_ref, bf16[1024,1024]{1,0:T(8,128)(2,1)} %bitcast.16, bf16[1024,1024]{1,0:T(8,128)(2,1)} %get-tuple-element.31.ctx_ref, ...), custom_call_target="tpu_custom_call" | custom-call | tf_op jit(solution)/shard_map/mlp_forward_backward/pallas_call | solution.py:389
  246.6 32.6 %attention_backward.1 = (bf16[1024,1024]{1,0:T(8,128)(2,1)}, bf16[1024,1024]{1,0:T(8,128)(2,1)}, bf16[1024,1024]{1,0:T(8,128)(2,1)}) custom-call(bf16[1024,3072]{1,0:T(8,128)(2,1)} %get-tuple-element.30.q_ref.k_ref.v_ref, bf16[1024,3072]{1,0:T(8,128)(2,1)} %get-tuple-element.30.q_ref.k_ref.v_ref, bf16[1024,3072]{1,0:T(8,128)(2,1)} %get-tuple-element.30.q_ref.k_ref.v_ref, ...), custom_call_target="tpu_custom_call" | custom-call | tf_op jit(solution)/shard_map/attention_backward/pallas_call | solution.py:317
  279.3 18.2 %tail_backward.1 = (bf16[1024,1024]{1,0:T(8,128)(2,1)}, bf16[8,144,128]{2,1,0:T(8,128)(2,1)}) custom-call(bf16[1024,1024]{1,0:T(8,128)(2,1)} %bitcast.17, f32[1024,1024]{1,0:T(8,128)} %get-tuple-element.36.gh_ref, bf16[1024,1024]{1,0:T(8,128)(2,1)} %get-tuple-element.37.normed_ref, bf16[1024,64]{1,0:T(8,128)(2,1)} %get-tuple-element.38.inner_ref, ...), custom_call_target="tpu_custom_call" | custom-call | tf_op jit(solution)/shard_map/tail_backward/pallas_call | solution.py:458
  297.5 25.9 %reduce_grads.1 = (f32[128,512]{1,0:T(8,128)}, f32[128,512]{1,0:T(8,128)}) custom-call(bf16[8,144,128]{2,1,0:T(8,128)(2,1)} %get-tuple-element.47.pay_ref), custom_call_target="tpu_custom_call" | custom-call | tf_op jit(solution)/shard_map/reduce_grads/pallas_call | solution.py:561
  323.4 1.7 copy.20
  325.0 1.7 copy.21
